TPU v7x, 256 devices: a whole 4x4x8 slice. The times are simulated.
256 devices in a mesh: row: 16 (over y, x), col: 16 (over z, core).
Axes of the slice: x: 4, y: 4, z: 8, core: 2. Of those that a mesh axis runs over, the one named last changes fastest.
Arguments:
- depth: float32 [1024, 8192], P('row', 'col'), may hold values from 0 to 1
- rainfall: float32 [1024, 8192], P('row', 'col'), may hold values from 0.05 to 0.5
- conveyance: float32 [1024, 8192], P('row', 'col'), may hold values from 0.2 to 5
- flow_dir: int32 [1024, 8192], P('row', 'col'), may hold values from 0 to 7, as said below
- outlet: int32 [1024, 8192], P('row', 'col'), may hold values 0 or 1
Outputs:
- new_depth: float32 [1024, 8192], P('row', 'col')
- discharge: float32 [1024, 8192], P('row', 'col')
Inputs may be any that keep to these rules, and one draw needn't show every extreme that they name: `flow_dir`: each cell's code is 0 to 7.
All inputs are finite; a program needn't handle non-finite values. No bound on the sum of `outlet` on one device may be relied on, other than what follows from the above.
Results may differ from a plain program's by a relative error of at most 0.00002.
Values sent between devices are 32-bit elements; how exact they have to be, the bound alone decides.
A program may use at most 64 MiB of HBM per device.

v0:
```python
import jax
import jax.numpy as jnp
from jax import lax
from jax.sharding import PartitionSpec as P

SUBSTEPS = 3
PASSES = 64


OFFSETS = ((0, 1), (1, 1), (1, 0), (1, -1), (0, -1), (-1, -1), (-1, 0), (-1, 1))


def extended(array, sides, width):
    for axis, dim in sides:
        peers, length = (lax.axis_size(axis), array.shape[dim])
        up = [(i, (i + 1) % peers) for i in range(peers - 1)]
        down = [(j, i) for i, j in up]
        last = lax.slice_in_dim(array, length - width, length, axis=dim)
        initial = lax.slice_in_dim(array, 0, width, axis=dim)
        before = lax.ppermute(last, axis, up)
        after = lax.ppermute(initial, axis, down)
        array = jnp.concatenate([before, array, after], axis=dim)
    return array


def padded_inflow(sent_pad, route_pad):
    rows = sent_pad.shape[0] - 2
    cols = sent_pad.shape[1] - 2
    total = jnp.zeros((rows, cols), jnp.float32)
    for k, (di, dj) in enumerate(OFFSETS):
        source = sent_pad[1 - di : 1 - di + rows, 1 - dj : 1 - dj + cols]
        target = route_pad[1 - di : 1 - di + rows, 1 - dj : 1 - dj + cols]
        total = total + jnp.where(target == k + 1, source, jnp.float32(0.0))
    return total


def on_device(depth, rainfall, conveyance, flow_dir, outlet):
    route = jnp.where(outlet == 1, 0, flow_dir + 1)
    length = jnp.where(flow_dir % 2 == 1, jnp.float32(0.70710678), jnp.float32(1.0))
    route_pad = extended(route, (("row", 0), ("col", 1)), 1)
    level = depth
    for step in range(SUBSTEPS):
        factor = conveyance * length * jnp.power(level, jnp.float32(2.0 / 3.0))
        share = factor / (1.0 + factor)
        out = level * share
        sent = jnp.where(route > 0, out, jnp.float32(0.0))
        sent_pad = extended(sent, (("row", 0), ("col", 1)), 1)
        level = level + rainfall - out + padded_inflow(sent_pad, route_pad)
    margin = 8
    route_wide = extended(route, (("row", 0), ("col", 1)), margin)
    level_wide = extended(level, (("row", 0), ("col", 1)), margin)
    rows, cols = level.shape

    def group_pass(index, acc):
        current = extended(acc, (("row", 0), ("col", 1)), margin)
        for inner in range(margin):
            edge = margin - inner
            route_here = route_wide[
                margin - edge : margin + rows + edge, margin - edge : margin + cols + edge
            ]
            level_here = level_wide[
                margin - edge + 1 : margin + rows + edge - 1,
                margin - edge + 1 : margin + cols + edge - 1,
            ]
            sent = jnp.where(route_here > 0, current, jnp.float32(0.0))
            current = level_here + padded_inflow(sent, route_here)
        return current

    acc = lax.fori_loop(0, PASSES // margin, group_pass, level)
    return (level, jnp.log(1.0 + acc))


def solution(mesh):
    placed = (P("row", "col"), P("row", "col"), P("row", "col"), P("row", "col"), P("row", "col"))
    return jax.shard_map(
        on_device,
        mesh=mesh,
        in_specs=placed,
        out_specs=(P("row", "col"), P("row", "col")),
        check_vma=False,
    )
```

profile of v0, /device:TPU:121, one launch (start us, length us, event | category | flops | bytes accessed | tf_op | source)
XLA Modules:
  0.0 297.6 jit_solution(5531393548171196123)
XLA Ops:
  0.6 1.4 broadcast_select_fusion.2
  2.0 3.1 %collective-permute-start.4 = (s32[1,512]{1,0:T(1,128)S(1)}, s32[1,512]{1,0:T(1,128)S(1)}, u32[]{:S(2)}, u32[]{:S(2)}) collective-permute-start(s32[1,512]{1,0:T(1,128)S(1)} %get-tuple-element.88), channel_id=1, source_target_pairs={{0,16},{16,32},{32,48},{48,64},{64,80},{80,96},{96,112},{112,128},... | collective-permute-start | bytes 6152 | tf_op jit(solution)/shard_map/ppermute | solution.py:20
  5.1 4.3 %collective-permute-start.5 = (s32[1,512]{1,0:T(1,128)S(1)}, s32[1,512]{1,0:T(1,128)S(1)}, u32[]{:S(2)}, u32[]{:S(2)}) collective-permute-start(s32[1,512]{1,0:T(1,128)S(1)} %get-tuple-element.89), channel_id=1, source_target_pairs={{16,0},{32,16},{48,32},{64,48},{80,64},{96,80},{112,96},{128,112},... | collective-permute-start | bytes 6152 | tf_op jit(solution)/shard_map/ppermute | solution.py:21
  9.4 1.9 collective-permute-start.7
  11.4 5.5 %collective-permute-start.8 = (f32[1,512]{1,0:T(1,128)S(1)}, f32[1,512]{1,0:T(1,128)S(1)}, u32[]{:S(2)}, u32[]{:S(2)}) collective-permute-start(f32[1,512]{1,0:T(1,128)S(1)} %get-tuple-element.91), channel_id=1, source_target_pairs={{16,0},{32,16},{48,32},{64,48},{80,64},{96,80},{112,96},{128,112},... | collective-permute-start | bytes 6152 | tf_op jit(solution)/shard_map/ppermute | solution.py:21
  16.9 3.7 %collective-permute-start.10 = (s32[66,1]{1,0:T(8,128)S(1)}, s32[66,1]{1,0:T(8,128)S(1)}, u32[]{:S(2)}, u32[]{:S(2)}) collective-permute-start(s32[66,1]{1,0:T(8,128)S(1)} %get-tuple-element.74), channel_id=1, source_target_pairs={{1,0},{2,1},{3,2},{4,3},{5,4},{6,5},{7,6},{8,7},{9,8},{10,9},{11,1... | collective-permute-start | bytes 800 | tf_op jit(solution)/shard_map/ppermute | solution.py:21
  20.6 4.7 %collective-permute-start.6 = (s32[66,1]{1,0:T(8,128)S(1)}, s32[66,1]{1,0:T(8,128)S(1)}, u32[]{:S(2)}, u32[]{:S(2)}) collective-permute-start(s32[66,1]{1,0:T(8,128)S(1)} %get-tuple-element.75), channel_id=1, source_target_pairs={{0,1},{1,2},{2,3},{3,4},{4,5},{5,6},{6,7},{7,8},{8,9},{9,10},{10,1... | collective-permute-start | bytes 800 | tf_op jit(solution)/shard_map/ppermute | solution.py:20
  25.4 1.9 collective-permute-start.11
  27.3 4.9 %collective-permute-start.9 = (f32[66,1]{1,0:T(8,128)S(1)}, f32[66,1]{1,0:T(8,128)S(1)}, u32[]{:S(2)}, u32[]{:S(2)}) collective-permute-start(f32[66,1]{1,0:T(8,128)S(1)} %get-tuple-element.79), channel_id=1, source_target_pairs={{0,1},{1,2},{2,3},{3,4},{4,5},{5,6},{6,7},{7,8},{8,9},{9,10},{10,1... | collective-permute-start | bytes 800 | tf_op jit(solution)/shard_map/ppermute | solution.py:20
  34.1 1.9 collective-permute-start.12
  36.1 5.5 %collective-permute-start.13 = (f32[1,512]{1,0:T(1,128)S(1)}, f32[1,512]{1,0:T(1,128)S(1)}, u32[]{:S(2)}, u32[]{:S(2)}) collective-permute-start(f32[1,512]{1,0:T(1,128)S(1)} %get-tuple-element.87), channel_id=1, source_target_pairs={{16,0},{32,16},{48,32},{64,48},{80,64},{96,80},{112,96},{128,112},... | collective-permute-start | bytes 6152 | tf_op jit(solution)/shard_map/ppermute | solution.py:21
  42.3 6.6 %collective-permute-start.14 = (f32[66,1]{1,0:T(8,128)S(1)}, f32[66,1]{1,0:T(8,128)S(1)}, u32[]{:S(2)}, u32[]{:S(2)}) collective-permute-start(f32[66,1]{1,0:T(8,128)S(1)} %get-tuple-element.71), channel_id=1, source_target_pairs={{0,1},{1,2},{2,3},{3,4},{4,5},{5,6},{6,7},{7,8},{8,9},{9,10},{10,1... | collective-permute-start | bytes 800 | tf_op jit(solution)/shard_map/ppermute | solution.py:20
  48.9 1.9 collective-permute-start.15
  50.8 4.5 %collective-permute-done.15 = f32[66,1]{1,0:T(8,128)S(1)} collective-permute-done((f32[66,1]{1,0:T(8,128)S(1)}, f32[66,1]{1,0:T(8,128)S(1)}, u32[]{:S(2)}, u32[]{:S(2)}) %collective-permute-start.15) | collective-permute-done | bytes 296 | tf_op jit(solution)/shard_map/ppermute | solution.py:21
  56.1 1.9 collective-permute-start.16
  58.1 6.0 %collective-permute-start.17 = (f32[1,512]{1,0:T(1,128)S(1)}, f32[1,512]{1,0:T(1,128)S(1)}, u32[]{:S(2)}, u32[]{:S(2)}) collective-permute-start(f32[1,512]{1,0:T(1,128)S(1)} %get-tuple-element.85), channel_id=1, source_target_pairs={{16,0},{32,16},{48,32},{64,48},{80,64},{96,80},{112,96},{128,112},... | collective-permute-start | bytes 6152 | tf_op jit(solution)/shard_map/ppermute | solution.py:21
  64.1 1.9 collective-permute-start.20
  66.1 2.2 collective-permute-start.18
  68.3 2.1 collective-permute-start.19
  70.5 5.5 %collective-permute-start.21 = (s32[8,512]{1,0:T(8,128)S(1)}, s32[8,512]{1,0:T(8,128)S(1)}, u32[]{:S(2)}, u32[]{:S(2)}) collective-permute-start(s32[8,512]{1,0:T(8,128)S(1)} %get-tuple-element.83), channel_id=1, source_target_pairs={{16,0},{32,16},{48,32},{64,48},{80,64},{96,80},{112,96},{128,112},... | collective-permute-start | bytes 49160 | tf_op jit(solution)/shard_map/ppermute | solution.py:21
  76.6 1.9 collective-permute-start.24
  78.5 5.5 %collective-permute-start.25 = (f32[8,512]{1,0:T(8,128)S(1)}, f32[8,512]{1,0:T(8,128)S(1)}, u32[]{:S(2)}, u32[]{:S(2)}) collective-permute-start(f32[8,512]{1,0:T(8,128)S(1)} %get-tuple-element.81), channel_id=1, source_target_pairs={{16,0},{32,16},{48,32},{64,48},{80,64},{96,80},{112,96},{128,112},... | collective-permute-start | bytes 49160 | tf_op jit(solution)/shard_map/ppermute | solution.py:21
  84.1 5.7 %collective-permute-start.22 = (s32[80,8]{1,0:T(8,128)S(1)}, s32[80,8]{1,0:T(8,128)S(1)}, u32[]{:S(2)}, u32[]{:S(2)}) collective-permute-start(s32[80,8]{1,0:T(8,128)S(1)} %get-tuple-element.62), channel_id=1, source_target_pairs={{0,1},{1,2},{2,3},{3,4},{4,5},{5,6},{6,7},{7,8},{8,9},{9,10},{10,1... | collective-permute-start | bytes 7688 | tf_op jit(solution)/shard_map/ppermute | solution.py:20
  89.8 1.9 collective-permute-start.23
  91.8 4.8 %collective-permute-start.26 = (f32[80,8]{1,0:T(8,128)S(1)}, f32[80,8]{1,0:T(8,128)S(1)}, u32[]{:S(2)}, u32[]{:S(2)}) collective-permute-start(f32[80,8]{1,0:T(8,128)S(1)} %get-tuple-element.60), channel_id=1, source_target_pairs={{0,1},{1,2},{2,3},{3,4},{4,5},{5,6},{6,7},{7,8},{8,9},{9,10},{10,1... | collective-permute-start | bytes 7688 | tf_op jit(solution)/shard_map/ppermute | solution.py:20
  96.7 1.9 collective-permute-start.27
  98.8 4.4 %collective-permute-done.27 = f32[80,8]{1,0:T(8,128)S(1)} collective-permute-done((f32[80,8]{1,0:T(8,128)S(1)}, f32[80,8]{1,0:T(8,128)S(1)}, u32[]{:S(2)}, u32[]{:S(2)}) %collective-permute-start.27) | collective-permute-done | bytes 2592 | tf_op jit(solution)/shard_map/ppermute | solution.py:21
  103.3 193.5 %while.10 = (s32[]{:T(128)}, f32[64,512]{1,0:T(8,128)S(1)}, s32[80,528]{1,0:T(8,128)S(1)}, f32[80,528]{1,0:T(8,128)S(1)}, f32[64,512]{1,0:T(8,128)S(1)}, /*index=5*/s32[]{:T(128)}) while((s32[]{:T(128)}, f32[64,512]{1,0:T(8,128)S(1)}, s32[80,528]{1,0:T(8,128)S(1)}, f32[80,528]{1,0:T(8,128)S(1)}, f32[64,512]{1,0:T(8,128)S(1)}, ...), condition=%wide.region_1.2_spmd, body=%wide.region_0.1_spmd.sunk | while | flops 7772386 | bytes 23348004 | solution.py:69
  103.4 1.9 collective-permute-start
  105.3 5.5 %collective-permute-start.1 = (f32[8,512]{1,0:T(8,128)S(1)}, f32[8,512]{1,0:T(8,128)S(1)}, u32[]{:S(2)}, u32[]{:S(2)}) collective-permute-start(f32[8,512]{1,0:T(8,128)S(1)} %get-tuple-element.128), channel_id=1, source_target_pairs={{16,0},{32,16},{48,32},{64,48},{80,64},{96,80},{112,96},{128,112},... | collective-permute-start | bytes 49160 | tf_op jit(solution)/shard_map/while/body/eval_jaxpr/ppermute | solution.py:21
  111.7 1.9 collective-permute-start.2
  113.6 4.9 %collective-permute-start.3 = (f32[80,8]{1,0:T(8,128)S(1)}, f32[80,8]{1,0:T(8,128)S(1)}, u32[]{:S(2)}, u32[]{:S(2)}) collective-permute-start(f32[80,8]{1,0:T(8,128)S(1)} %get-tuple-element.130), channel_id=1, source_target_pairs={{0,1},{1,2},{2,3},{3,4},{4,5},{5,6},{6,7},{7,8},{8,9},{9,10},{10,1... | collective-permute-start | bytes 7688 | tf_op jit(solution)/shard_map/while/body/eval_jaxpr/ppermute | solution.py:20
  118.5 1.1 collective-permute-done.3
  125.8 1.9 collective-permute-start
  127.8 5.7 %collective-permute-start.1 = (f32[8,512]{1,0:T(8,128)S(1)}, f32[8,512]{1,0:T(8,128)S(1)}, u32[]{:S(2)}, u32[]{:S(2)}) collective-permute-start(f32[8,512]{1,0:T(8,128)S(1)} %get-tuple-element.128), channel_id=1, source_target_pairs={{16,0},{32,16},{48,32},{64,48},{80,64},{96,80},{112,96},{128,112},... | collective-permute-start | bytes 49160 | tf_op jit(solution)/shard_map/while/body/eval_jaxpr/ppermute | solution.py:21
  134.4 1.9 collective-permute-start.2
  136.3 6.3 %collective-permute-start.3 = (f32[80,8]{1,0:T(8,128)S(1)}, f32[80,8]{1,0:T(8,128)S(1)}, u32[]{:S(2)}, u32[]{:S(2)}) collective-permute-start(f32[80,8]{1,0:T(8,128)S(1)} %get-tuple-element.130), channel_id=1, source_target_pairs={{0,1},{1,2},{2,3},{3,4},{4,5},{5,6},{6,7},{7,8},{8,9},{9,10},{10,1... | collective-permute-start | bytes 7688 | tf_op jit(solution)/shard_map/while/body/eval_jaxpr/ppermute | solution.py:20
  142.7 1.1 collective-permute-done.3
  150.0 1.9 collective-permute-start
  151.9 6.0 %collective-permute-start.1 = (f32[8,512]{1,0:T(8,128)S(1)}, f32[8,512]{1,0:T(8,128)S(1)}, u32[]{:S(2)}, u32[]{:S(2)}) collective-permute-start(f32[8,512]{1,0:T(8,128)S(1)} %get-tuple-element.128), channel_id=1, source_target_pairs={{16,0},{32,16},{48,32},{64,48},{80,64},{96,80},{112,96},{128,112},... | collective-permute-start | bytes 49160 | tf_op jit(solution)/shard_map/while/body/eval_jaxpr/ppermute | solution.py:21
  158.9 1.9 collective-permute-start.2
  160.8 6.3 %collective-permute-start.3 = (f32[80,8]{1,0:T(8,128)S(1)}, f32[80,8]{1,0:T(8,128)S(1)}, u32[]{:S(2)}, u32[]{:S(2)}) collective-permute-start(f32[80,8]{1,0:T(8,128)S(1)} %get-tuple-element.130), channel_id=1, source_target_pairs={{0,1},{1,2},{2,3},{3,4},{4,5},{5,6},{6,7},{7,8},{8,9},{9,10},{10,1... | collective-permute-start | bytes 7688 | tf_op jit(solution)/shard_map/while/body/eval_jaxpr/ppermute | solution.py:20
  167.2 1.1 collective-permute-done.3
  174.5 1.9 collective-permute-start
  176.4 6.0 %collective-permute-start.1 = (f32[8,512]{1,0:T(8,128)S(1)}, f32[8,512]{1,0:T(8,128)S(1)}, u32[]{:S(2)}, u32[]{:S(2)}) collective-permute-start(f32[8,512]{1,0:T(8,128)S(1)} %get-tuple-element.128), channel_id=1, source_target_pairs={{16,0},{32,16},{48,32},{64,48},{80,64},{96,80},{112,96},{128,112},... | collective-permute-start | bytes 49160 | tf_op jit(solution)/shard_map/while/body/eval_jaxpr/ppermute | solution.py:21
  183.4 1.9 collective-permute-start.2
  185.3 6.3 %collective-permute-start.3 = (f32[80,8]{1,0:T(8,128)S(1)}, f32[80,8]{1,0:T(8,128)S(1)}, u32[]{:S(2)}, u32[]{:S(2)}) collective-permute-start(f32[80,8]{1,0:T(8,128)S(1)} %get-tuple-element.130), channel_id=1, source_target_pairs={{0,1},{1,2},{2,3},{3,4},{4,5},{5,6},{6,7},{7,8},{8,9},{9,10},{10,1... | collective-permute-start | bytes 7688 | tf_op jit(solution)/shard_map/while/body/eval_jaxpr/ppermute | solution.py:20
  191.6 1.1 collective-permute-done.3
  199.0 1.9 collective-permute-start
  200.9 6.0 %collective-permute-start.1 = (f32[8,512]{1,0:T(8,128)S(1)}, f32[8,512]{1,0:T(8,128)S(1)}, u32[]{:S(2)}, u32[]{:S(2)}) collective-permute-start(f32[8,512]{1,0:T(8,128)S(1)} %get-tuple-element.128), channel_id=1, source_target_pairs={{16,0},{32,16},{48,32},{64,48},{80,64},{96,80},{112,96},{128,112},... | collective-permute-start | bytes 49160 | tf_op jit(solution)/shard_map/while/body/eval_jaxpr/ppermute | solution.py:21
  207.9 1.9 collective-permute-start.2
  209.8 6.3 %collective-permute-start.3 = (f32[80,8]{1,0:T(8,128)S(1)}, f32[80,8]{1,0:T(8,128)S(1)}, u32[]{:S(2)}, u32[]{:S(2)}) collective-permute-start(f32[80,8]{1,0:T(8,128)S(1)} %get-tuple-element.130), channel_id=1, source_target_pairs={{0,1},{1,2},{2,3},{3,4},{4,5},{5,6},{6,7},{7,8},{8,9},{9,10},{10,1... | collective-permute-start | bytes 7688 | tf_op jit(solution)/shard_map/while/body/eval_jaxpr/ppermute | solution.py:20
  223.5 1.9 collective-permute-start
  225.4 6.0 %collective-permute-start.1 = (f32[8,512]{1,0:T(8,128)S(1)}, f32[8,512]{1,0:T(8,128)S(1)}, u32[]{:S(2)}, u32[]{:S(2)}) collective-permute-start(f32[8,512]{1,0:T(8,128)S(1)} %get-tuple-element.128), channel_id=1, source_target_pairs={{16,0},{32,16},{48,32},{64,48},{80,64},{96,80},{112,96},{128,112},... | collective-permute-start | bytes 49160 | tf_op jit(solution)/shard_map/while/body/eval_jaxpr/ppermute | solution.py:21
  232.3 1.9 collective-permute-start.2
  234.3 6.3 %collective-permute-start.3 = (f32[80,8]{1,0:T(8,128)S(1)}, f32[80,8]{1,0:T(8,128)S(1)}, u32[]{:S(2)}, u32[]{:S(2)}) collective-permute-start(f32[80,8]{1,0:T(8,128)S(1)} %get-tuple-element.130), channel_id=1, source_target_pairs={{0,1},{1,2},{2,3},{3,4},{4,5},{5,6},{6,7},{7,8},{8,9},{9,10},{10,1... | collective-permute-start | bytes 7688 | tf_op jit(solution)/shard_map/while/body/eval_jaxpr/ppermute | solution.py:20
  247.9 1.9 collective-permute-start
  249.9 6.0 %collective-permute-start.1 = (f32[8,512]{1,0:T(8,128)S(1)}, f32[8,512]{1,0:T(8,128)S(1)}, u32[]{:S(2)}, u32[]{:S(2)}) collective-permute-start(f32[8,512]{1,0:T(8,128)S(1)} %get-tuple-element.128), channel_id=1, source_target_pairs={{16,0},{32,16},{48,32},{64,48},{80,64},{96,80},{112,96},{128,112},... | collective-permute-start | bytes 49160 | tf_op jit(solution)/shard_map/while/body/eval_jaxpr/ppermute | solution.py:21
  256.8 1.9 collective-permute-start.2
  258.7 6.3 %collective-permute-start.3 = (f32[80,8]{1,0:T(8,128)S(1)}, f32[80,8]{1,0:T(8,128)S(1)}, u32[]{:S(2)}, u32[]{:S(2)}) collective-permute-start(f32[80,8]{1,0:T(8,128)S(1)} %get-tuple-element.130), channel_id=1, source_target_pairs={{0,1},{1,2},{2,3},{3,4},{4,5},{5,6},{6,7},{7,8},{8,9},{9,10},{10,1... | collective-permute-start | bytes 7688 | tf_op jit(solution)/shard_map/while/body/eval_jaxpr/ppermute | solution.py:20
  272.4 1.9 collective-permute-start
  274.3 6.0 %collective-permute-start.1 = (f32[8,512]{1,0:T(8,128)S(1)}, f32[8,512]{1,0:T(8,128)S(1)}, u32[]{:S(2)}, u32[]{:S(2)}) collective-permute-start(f32[8,512]{1,0:T(8,128)S(1)} %get-tuple-element.128), channel_id=1, source_target_pairs={{16,0},{32,16},{48,32},{64,48},{80,64},{96,80},{112,96},{128,112},... | collective-permute-start | bytes 49160 | tf_op jit(solution)/shard_map/while/body/eval_jaxpr/ppermute | solution.py:21
  281.3 1.9 collective-permute-start.2
  283.2 6.3 %collective-permute-start.3 = (f32[80,8]{1,0:T(8,128)S(1)}, f32[80,8]{1,0:T(8,128)S(1)}, u32[]{:S(2)}, u32[]{:S(2)}) collective-permute-start(f32[80,8]{1,0:T(8,128)S(1)} %get-tuple-element.130), channel_id=1, source_target_pairs={{0,1},{1,2},{2,3},{3,4},{4,5},{5,6},{6,7},{7,8},{8,9},{9,10},{10,1... | collective-permute-start | bytes 7688 | tf_op jit(solution)/shard_map/while/body/eval_jaxpr/ppermute | solution.py:20
  (191 shorter events, 66.3 us)
Async XLA Ops:
  2.0 14.8 %collective-permute-start.4 = (s32[1,512]{1,0:T(1,128)S(1)}, s32[1,512]{1,0:T(1,128)S(1)}, u32[]{:S(2)}, u32[]{:S(2)}) collective-permute-start(s32[1,512]{1,0:T(1,128)S(1)} %get-tuple-element.88), channel_id=1, source_target_pairs={{0,16},{16,32},{32,48},{48,64},{64,80},{80,96},{96,112},{112,128},... | collective-permute-start | bytes 6152 | tf_op jit(solution)/shard_map/ppermute | solution.py:20
  5.1 11.7 %collective-permute-start.5 = (s32[1,512]{1,0:T(1,128)S(1)}, s32[1,512]{1,0:T(1,128)S(1)}, u32[]{:S(2)}, u32[]{:S(2)}) collective-permute-start(s32[1,512]{1,0:T(1,128)S(1)} %get-tuple-element.89), channel_id=1, source_target_pairs={{16,0},{32,16},{48,32},{64,48},{80,64},{96,80},{112,96},{128,112},... | collective-permute-start | bytes 6152 | tf_op jit(solution)/shard_map/ppermute | solution.py:21
  9.4 15.9 %collective-permute-start.7 = (f32[1,512]{1,0:T(1,128)S(1)}, f32[1,512]{1,0:T(1,128)S(1)}, u32[]{:S(2)}, u32[]{:S(2)}) collective-permute-start(f32[1,512]{1,0:T(1,128)S(1)} %get-tuple-element.90), channel_id=1, source_target_pairs={{0,16},{16,32},{32,48},{48,64},{64,80},{80,96},{96,112},{112,128},... | collective-permute-start | bytes 6152 | tf_op jit(solution)/shard_map/ppermute | solution.py:20
  11.4 14.0 %collective-permute-start.8 = (f32[1,512]{1,0:T(1,128)S(1)}, f32[1,512]{1,0:T(1,128)S(1)}, u32[]{:S(2)}, u32[]{:S(2)}) collective-permute-start(f32[1,512]{1,0:T(1,128)S(1)} %get-tuple-element.91), channel_id=1, source_target_pairs={{16,0},{32,16},{48,32},{64,48},{80,64},{96,80},{112,96},{128,112},... | collective-permute-start | bytes 6152 | tf_op jit(solution)/shard_map/ppermute | solution.py:21
  16.9 15.3 %collective-permute-start.10 = (s32[66,1]{1,0:T(8,128)S(1)}, s32[66,1]{1,0:T(8,128)S(1)}, u32[]{:S(2)}, u32[]{:S(2)}) collective-permute-start(s32[66,1]{1,0:T(8,128)S(1)} %get-tuple-element.74), channel_id=1, source_target_pairs={{1,0},{2,1},{3,2},{4,3},{5,4},{6,5},{7,6},{8,7},{9,8},{10,9},{11,1... | collective-permute-start | bytes 800 | tf_op jit(solution)/shard_map/ppermute | solution.py:21
  20.6 11.6 %collective-permute-start.6 = (s32[66,1]{1,0:T(8,128)S(1)}, s32[66,1]{1,0:T(8,128)S(1)}, u32[]{:S(2)}, u32[]{:S(2)}) collective-permute-start(s32[66,1]{1,0:T(8,128)S(1)} %get-tuple-element.75), channel_id=1, source_target_pairs={{0,1},{1,2},{2,3},{3,4},{4,5},{5,6},{6,7},{7,8},{8,9},{9,10},{10,1... | collective-permute-start | bytes 800 | tf_op jit(solution)/shard_map/ppermute | solution.py:20
  25.4 7.0 %collective-permute-start.11 = (f32[66,1]{1,0:T(8,128)S(1)}, f32[66,1]{1,0:T(8,128)S(1)}, u32[]{:S(2)}, u32[]{:S(2)}) collective-permute-start(f32[66,1]{1,0:T(8,128)S(1)} %get-tuple-element.78), channel_id=1, source_target_pairs={{1,0},{2,1},{3,2},{4,3},{5,4},{6,5},{7,6},{8,7},{9,8},{10,9},{11,1... | collective-permute-start | bytes 800 | tf_op jit(solution)/shard_map/ppermute | solution.py:21
  27.3 5.9 %collective-permute-start.9 = (f32[66,1]{1,0:T(8,128)S(1)}, f32[66,1]{1,0:T(8,128)S(1)}, u32[]{:S(2)}, u32[]{:S(2)}) collective-permute-start(f32[66,1]{1,0:T(8,128)S(1)} %get-tuple-element.79), channel_id=1, source_target_pairs={{0,1},{1,2},{2,3},{3,4},{4,5},{5,6},{6,7},{7,8},{8,9},{9,10},{10,1... | collective-permute-start | bytes 800 | tf_op jit(solution)/shard_map/ppermute | solution.py:20
  32.3 1.0 copy-start.1
  32.4 1.0 copy-start.2
  34.1 7.4 %collective-permute-start.12 = (f32[1,512]{1,0:T(1,128)S(1)}, f32[1,512]{1,0:T(1,128)S(1)}, u32[]{:S(2)}, u32[]{:S(2)}) collective-permute-start(f32[1,512]{1,0:T(1,128)S(1)} %get-tuple-element.86), channel_id=1, source_target_pairs={{0,16},{16,32},{32,48},{48,64},{64,80},{80,96},{96,112},{112,128},... | collective-permute-start | bytes 6152 | tf_op jit(solution)/shard_map/ppermute | solution.py:20
  36.1 6.2 %collective-permute-start.13 = (f32[1,512]{1,0:T(1,128)S(1)}, f32[1,512]{1,0:T(1,128)S(1)}, u32[]{:S(2)}, u32[]{:S(2)}) collective-permute-start(f32[1,512]{1,0:T(1,128)S(1)} %get-tuple-element.87), channel_id=1, source_target_pairs={{16,0},{32,16},{48,32},{64,48},{80,64},{96,80},{112,96},{128,112},... | collective-permute-start | bytes 6152 | tf_op jit(solution)/shard_map/ppermute | solution.py:21
  42.3 8.5 %collective-permute-start.14 = (f32[66,1]{1,0:T(8,128)S(1)}, f32[66,1]{1,0:T(8,128)S(1)}, u32[]{:S(2)}, u32[]{:S(2)}) collective-permute-start(f32[66,1]{1,0:T(8,128)S(1)} %get-tuple-element.71), channel_id=1, source_target_pairs={{0,1},{1,2},{2,3},{3,4},{4,5},{5,6},{6,7},{7,8},{8,9},{9,10},{10,1... | collective-permute-start | bytes 800 | tf_op jit(solution)/shard_map/ppermute | solution.py:20
  48.9 6.5 %collective-permute-start.15 = (f32[66,1]{1,0:T(8,128)S(1)}, f32[66,1]{1,0:T(8,128)S(1)}, u32[]{:S(2)}, u32[]{:S(2)}) collective-permute-start(f32[66,1]{1,0:T(8,128)S(1)} %get-tuple-element.70), channel_id=1, source_target_pairs={{1,0},{2,1},{3,2},{4,3},{5,4},{6,5},{7,6},{8,7},{9,8},{10,9},{11,1... | collective-permute-start | bytes 800 | tf_op jit(solution)/shard_map/ppermute | solution.py:21
  56.1 9.9 %collective-permute-start.16 = (f32[1,512]{1,0:T(1,128)S(1)}, f32[1,512]{1,0:T(1,128)S(1)}, u32[]{:S(2)}, u32[]{:S(2)}) collective-permute-start(f32[1,512]{1,0:T(1,128)S(1)} %get-tuple-element.84), channel_id=1, source_target_pairs={{0,16},{16,32},{32,48},{48,64},{64,80},{80,96},{96,112},{112,128},... | collective-permute-start | bytes 6152 | tf_op jit(solution)/shard_map/ppermute | solution.py:20
  58.1 8.0 %collective-permute-start.17 = (f32[1,512]{1,0:T(1,128)S(1)}, f32[1,512]{1,0:T(1,128)S(1)}, u32[]{:S(2)}, u32[]{:S(2)}) collective-permute-start(f32[1,512]{1,0:T(1,128)S(1)} %get-tuple-element.85), channel_id=1, source_target_pairs={{16,0},{32,16},{48,32},{64,48},{80,64},{96,80},{112,96},{128,112},... | collective-permute-start | bytes 6152 | tf_op jit(solution)/shard_map/ppermute | solution.py:21
  64.1 19.9 %collective-permute-start.20 = (s32[8,512]{1,0:T(8,128)S(1)}, s32[8,512]{1,0:T(8,128)S(1)}, u32[]{:S(2)}, u32[]{:S(2)}) collective-permute-start(s32[8,512]{1,0:T(8,128)S(1)} %get-tuple-element.82), channel_id=1, source_target_pairs={{0,16},{16,32},{32,48},{48,64},{64,80},{80,96},{96,112},{112,128},... | collective-permute-start | bytes 49160 | tf_op jit(solution)/shard_map/ppermute | solution.py:20
  66.1 9.9 %collective-permute-start.18 = (f32[66,1]{1,0:T(8,128)S(1)}, f32[66,1]{1,0:T(8,128)S(1)}, u32[]{:S(2)}, u32[]{:S(2)}) collective-permute-start(f32[66,1]{1,0:T(8,128)S(1)} %get-tuple-element.67), channel_id=1, source_target_pairs={{0,1},{1,2},{2,3},{3,4},{4,5},{5,6},{6,7},{7,8},{8,9},{9,10},{10,1... | collective-permute-start | bytes 800 | tf_op jit(solution)/shard_map/ppermute | solution.py:20
  68.3 7.7 %collective-permute-start.19 = (f32[66,1]{1,0:T(8,128)S(1)}, f32[66,1]{1,0:T(8,128)S(1)}, u32[]{:S(2)}, u32[]{:S(2)}) collective-permute-start(f32[66,1]{1,0:T(8,128)S(1)} %get-tuple-element.66), channel_id=1, source_target_pairs={{1,0},{2,1},{3,2},{4,3},{5,4},{6,5},{7,6},{8,7},{9,8},{10,9},{11,1... | collective-permute-start | bytes 800 | tf_op jit(solution)/shard_map/ppermute | solution.py:21
  70.5 13.5 %collective-permute-start.21 = (s32[8,512]{1,0:T(8,128)S(1)}, s32[8,512]{1,0:T(8,128)S(1)}, u32[]{:S(2)}, u32[]{:S(2)}) collective-permute-start(s32[8,512]{1,0:T(8,128)S(1)} %get-tuple-element.83), channel_id=1, source_target_pairs={{16,0},{32,16},{48,32},{64,48},{80,64},{96,80},{112,96},{128,112},... | collective-permute-start | bytes 49160 | tf_op jit(solution)/shard_map/ppermute | solution.py:21
  76.6 15.1 %collective-permute-start.24 = (f32[8,512]{1,0:T(8,128)S(1)}, f32[8,512]{1,0:T(8,128)S(1)}, u32[]{:S(2)}, u32[]{:S(2)}) collective-permute-start(f32[8,512]{1,0:T(8,128)S(1)} %get-tuple-element.80), channel_id=1, source_target_pairs={{0,16},{16,32},{32,48},{48,64},{64,80},{80,96},{96,112},{112,128},... | collective-permute-start | bytes 49160 | tf_op jit(solution)/shard_map/ppermute | solution.py:20
  78.5 13.2 %collective-permute-start.25 = (f32[8,512]{1,0:T(8,128)S(1)}, f32[8,512]{1,0:T(8,128)S(1)}, u32[]{:S(2)}, u32[]{:S(2)}) collective-permute-start(f32[8,512]{1,0:T(8,128)S(1)} %get-tuple-element.81), channel_id=1, source_target_pairs={{16,0},{32,16},{48,32},{64,48},{80,64},{96,80},{112,96},{128,112},... | collective-permute-start | bytes 49160 | tf_op jit(solution)/shard_map/ppermute | solution.py:21
  84.1 14.5 %collective-permute-start.22 = (s32[80,8]{1,0:T(8,128)S(1)}, s32[80,8]{1,0:T(8,128)S(1)}, u32[]{:S(2)}, u32[]{:S(2)}) collective-permute-start(s32[80,8]{1,0:T(8,128)S(1)} %get-tuple-element.62), channel_id=1, source_target_pairs={{0,1},{1,2},{2,3},{3,4},{4,5},{5,6},{6,7},{7,8},{8,9},{9,10},{10,1... | collective-permute-start | bytes 7688 | tf_op jit(solution)/shard_map/ppermute | solution.py:20
  89.8 8.8 %collective-permute-start.23 = (s32[80,8]{1,0:T(8,128)S(1)}, s32[80,8]{1,0:T(8,128)S(1)}, u32[]{:S(2)}, u32[]{:S(2)}) collective-permute-start(s32[80,8]{1,0:T(8,128)S(1)} %get-tuple-element.63), channel_id=1, source_target_pairs={{1,0},{2,1},{3,2},{4,3},{5,4},{6,5},{7,6},{8,7},{9,8},{10,9},{11,1... | collective-permute-start | bytes 7688 | tf_op jit(solution)/shard_map/ppermute | solution.py:21
  91.8 6.9 %collective-permute-start.26 = (f32[80,8]{1,0:T(8,128)S(1)}, f32[80,8]{1,0:T(8,128)S(1)}, u32[]{:S(2)}, u32[]{:S(2)}) collective-permute-start(f32[80,8]{1,0:T(8,128)S(1)} %get-tuple-element.60), channel_id=1, source_target_pairs={{0,1},{1,2},{2,3},{3,4},{4,5},{5,6},{6,7},{7,8},{8,9},{9,10},{10,1... | collective-permute-start | bytes 7688 | tf_op jit(solution)/shard_map/ppermute | solution.py:20
  96.7 6.5 %collective-permute-start.27 = (f32[80,8]{1,0:T(8,128)S(1)}, f32[80,8]{1,0:T(8,128)S(1)}, u32[]{:S(2)}, u32[]{:S(2)}) collective-permute-start(f32[80,8]{1,0:T(8,128)S(1)} %get-tuple-element.61), channel_id=1, source_target_pairs={{1,0},{2,1},{3,2},{4,3},{5,4},{6,5},{7,6},{8,7},{9,8},{10,9},{11,1... | collective-permute-start | bytes 7688 | tf_op jit(solution)/shard_map/ppermute | solution.py:21
  103.4 7.4 %collective-permute-start = (f32[8,512]{1,0:T(8,128)S(1)}, f32[8,512]{1,0:T(8,128)S(1)}, u32[]{:S(2)}, u32[]{:S(2)}) collective-permute-start(f32[8,512]{1,0:T(8,128)S(1)} %get-tuple-element.127), channel_id=1, source_target_pairs={{0,16},{16,32},{32,48},{48,64},{64,80},{80,96},{96,112},{112,128},... | collective-permute-start | bytes 49160 | tf_op jit(solution)/shard_map/while/body/eval_jaxpr/ppermute | solution.py:20
  105.3 6.3 %collective-permute-start.1 = (f32[8,512]{1,0:T(8,128)S(1)}, f32[8,512]{1,0:T(8,128)S(1)}, u32[]{:S(2)}, u32[]{:S(2)}) collective-permute-start(f32[8,512]{1,0:T(8,128)S(1)} %get-tuple-element.128), channel_id=1, source_target_pairs={{16,0},{32,16},{48,32},{64,48},{80,64},{96,80},{112,96},{128,112},... | collective-permute-start | bytes 49160 | tf_op jit(solution)/shard_map/while/body/eval_jaxpr/ppermute | solution.py:21
  111.7 6.8 %collective-permute-start.2 = (f32[80,8]{1,0:T(8,128)S(1)}, f32[80,8]{1,0:T(8,128)S(1)}, u32[]{:S(2)}, u32[]{:S(2)}) collective-permute-start(f32[80,8]{1,0:T(8,128)S(1)} %get-tuple-element.129), channel_id=1, source_target_pairs={{1,0},{2,1},{3,2},{4,3},{5,4},{6,5},{7,6},{8,7},{9,8},{10,9},{11,1... | collective-permute-start | bytes 7688 | tf_op jit(solution)/shard_map/while/body/eval_jaxpr/ppermute | solution.py:21
  113.6 5.9 %collective-permute-start.3 = (f32[80,8]{1,0:T(8,128)S(1)}, f32[80,8]{1,0:T(8,128)S(1)}, u32[]{:S(2)}, u32[]{:S(2)}) collective-permute-start(f32[80,8]{1,0:T(8,128)S(1)} %get-tuple-element.130), channel_id=1, source_target_pairs={{0,1},{1,2},{2,3},{3,4},{4,5},{5,6},{6,7},{7,8},{8,9},{9,10},{10,1... | collective-permute-start | bytes 7688 | tf_op jit(solution)/shard_map/while/body/eval_jaxpr/ppermute | solution.py:20
  125.8 7.7 %collective-permute-start = (f32[8,512]{1,0:T(8,128)S(1)}, f32[8,512]{1,0:T(8,128)S(1)}, u32[]{:S(2)}, u32[]{:S(2)}) collective-permute-start(f32[8,512]{1,0:T(8,128)S(1)} %get-tuple-element.127), channel_id=1, source_target_pairs={{0,16},{16,32},{32,48},{48,64},{64,80},{80,96},{96,112},{112,128},... | collective-permute-start | bytes 49160 | tf_op jit(solution)/shard_map/while/body/eval_jaxpr/ppermute | solution.py:20
  127.8 6.6 %collective-permute-start.1 = (f32[8,512]{1,0:T(8,128)S(1)}, f32[8,512]{1,0:T(8,128)S(1)}, u32[]{:S(2)}, u32[]{:S(2)}) collective-permute-start(f32[8,512]{1,0:T(8,128)S(1)} %get-tuple-element.128), channel_id=1, source_target_pairs={{16,0},{32,16},{48,32},{64,48},{80,64},{96,80},{112,96},{128,112},... | collective-permute-start | bytes 49160 | tf_op jit(solution)/shard_map/while/body/eval_jaxpr/ppermute | solution.py:21
  134.4 8.2 %collective-permute-start.2 = (f32[80,8]{1,0:T(8,128)S(1)}, f32[80,8]{1,0:T(8,128)S(1)}, u32[]{:S(2)}, u32[]{:S(2)}) collective-permute-start(f32[80,8]{1,0:T(8,128)S(1)} %get-tuple-element.129), channel_id=1, source_target_pairs={{1,0},{2,1},{3,2},{4,3},{5,4},{6,5},{7,6},{8,7},{9,8},{10,9},{11,1... | collective-permute-start | bytes 7688 | tf_op jit(solution)/shard_map/while/body/eval_jaxpr/ppermute | solution.py:21
  136.3 7.4 %collective-permute-start.3 = (f32[80,8]{1,0:T(8,128)S(1)}, f32[80,8]{1,0:T(8,128)S(1)}, u32[]{:S(2)}, u32[]{:S(2)}) collective-permute-start(f32[80,8]{1,0:T(8,128)S(1)} %get-tuple-element.130), channel_id=1, source_target_pairs={{0,1},{1,2},{2,3},{3,4},{4,5},{5,6},{6,7},{7,8},{8,9},{9,10},{10,1... | collective-permute-start | bytes 7688 | tf_op jit(solution)/shard_map/while/body/eval_jaxpr/ppermute | solution.py:20
  150.0 8.0 %collective-permute-start = (f32[8,512]{1,0:T(8,128)S(1)}, f32[8,512]{1,0:T(8,128)S(1)}, u32[]{:S(2)}, u32[]{:S(2)}) collective-permute-start(f32[8,512]{1,0:T(8,128)S(1)} %get-tuple-element.127), channel_id=1, source_target_pairs={{0,16},{16,32},{32,48},{48,64},{64,80},{80,96},{96,112},{112,128},... | collective-permute-start | bytes 49160 | tf_op jit(solution)/shard_map/while/body/eval_jaxpr/ppermute | solution.py:20
  151.9 6.9 %collective-permute-start.1 = (f32[8,512]{1,0:T(8,128)S(1)}, f32[8,512]{1,0:T(8,128)S(1)}, u32[]{:S(2)}, u32[]{:S(2)}) collective-permute-start(f32[8,512]{1,0:T(8,128)S(1)} %get-tuple-element.128), channel_id=1, source_target_pairs={{16,0},{32,16},{48,32},{64,48},{80,64},{96,80},{112,96},{128,112},... | collective-permute-start | bytes 49160 | tf_op jit(solution)/shard_map/while/body/eval_jaxpr/ppermute | solution.py:21
  158.9 8.2 %collective-permute-start.2 = (f32[80,8]{1,0:T(8,128)S(1)}, f32[80,8]{1,0:T(8,128)S(1)}, u32[]{:S(2)}, u32[]{:S(2)}) collective-permute-start(f32[80,8]{1,0:T(8,128)S(1)} %get-tuple-element.129), channel_id=1, source_target_pairs={{1,0},{2,1},{3,2},{4,3},{5,4},{6,5},{7,6},{8,7},{9,8},{10,9},{11,1... | collective-permute-start | bytes 7688 | tf_op jit(solution)/shard_map/while/body/eval_jaxpr/ppermute | solution.py:21
  160.8 7.4 %collective-permute-start.3 = (f32[80,8]{1,0:T(8,128)S(1)}, f32[80,8]{1,0:T(8,128)S(1)}, u32[]{:S(2)}, u32[]{:S(2)}) collective-permute-start(f32[80,8]{1,0:T(8,128)S(1)} %get-tuple-element.130), channel_id=1, source_target_pairs={{0,1},{1,2},{2,3},{3,4},{4,5},{5,6},{6,7},{7,8},{8,9},{9,10},{10,1... | collective-permute-start | bytes 7688 | tf_op jit(solution)/shard_map/while/body/eval_jaxpr/ppermute | solution.py:20
  174.5 8.0 %collective-permute-start = (f32[8,512]{1,0:T(8,128)S(1)}, f32[8,512]{1,0:T(8,128)S(1)}, u32[]{:S(2)}, u32[]{:S(2)}) collective-permute-start(f32[8,512]{1,0:T(8,128)S(1)} %get-tuple-element.127), channel_id=1, source_target_pairs={{0,16},{16,32},{32,48},{48,64},{64,80},{80,96},{96,112},{112,128},... | collective-permute-start | bytes 49160 | tf_op jit(solution)/shard_map/while/body/eval_jaxpr/ppermute | solution.py:20
  176.4 6.9 %collective-permute-start.1 = (f32[8,512]{1,0:T(8,128)S(1)}, f32[8,512]{1,0:T(8,128)S(1)}, u32[]{:S(2)}, u32[]{:S(2)}) collective-permute-start(f32[8,512]{1,0:T(8,128)S(1)} %get-tuple-element.128), channel_id=1, source_target_pairs={{16,0},{32,16},{48,32},{64,48},{80,64},{96,80},{112,96},{128,112},... | collective-permute-start | bytes 49160 | tf_op jit(solution)/shard_map/while/body/eval_jaxpr/ppermute | solution.py:21
  183.4 8.2 %collective-permute-start.2 = (f32[80,8]{1,0:T(8,128)S(1)}, f32[80,8]{1,0:T(8,128)S(1)}, u32[]{:S(2)}, u32[]{:S(2)}) collective-permute-start(f32[80,8]{1,0:T(8,128)S(1)} %get-tuple-element.129), channel_id=1, source_target_pairs={{1,0},{2,1},{3,2},{4,3},{5,4},{6,5},{7,6},{8,7},{9,8},{10,9},{11,1... | collective-permute-start | bytes 7688 | tf_op jit(solution)/shard_map/while/body/eval_jaxpr/ppermute | solution.py:21
  185.3 7.4 %collective-permute-start.3 = (f32[80,8]{1,0:T(8,128)S(1)}, f32[80,8]{1,0:T(8,128)S(1)}, u32[]{:S(2)}, u32[]{:S(2)}) collective-permute-start(f32[80,8]{1,0:T(8,128)S(1)} %get-tuple-element.130), channel_id=1, source_target_pairs={{0,1},{1,2},{2,3},{3,4},{4,5},{5,6},{6,7},{7,8},{8,9},{9,10},{10,1... | collective-permute-start | bytes 7688 | tf_op jit(solution)/shard_map/while/body/eval_jaxpr/ppermute | solution.py:20
  199.0 8.0 %collective-permute-start = (f32[8,512]{1,0:T(8,128)S(1)}, f32[8,512]{1,0:T(8,128)S(1)}, u32[]{:S(2)}, u32[]{:S(2)}) collective-permute-start(f32[8,512]{1,0:T(8,128)S(1)} %get-tuple-element.127), channel_id=1, source_target_pairs={{0,16},{16,32},{32,48},{48,64},{64,80},{80,96},{96,112},{112,128},... | collective-permute-start | bytes 49160 | tf_op jit(solution)/shard_map/while/body/eval_jaxpr/ppermute | solution.py:20
  200.9 6.9 %collective-permute-start.1 = (f32[8,512]{1,0:T(8,128)S(1)}, f32[8,512]{1,0:T(8,128)S(1)}, u32[]{:S(2)}, u32[]{:S(2)}) collective-permute-start(f32[8,512]{1,0:T(8,128)S(1)} %get-tuple-element.128), channel_id=1, source_target_pairs={{16,0},{32,16},{48,32},{64,48},{80,64},{96,80},{112,96},{128,112},... | collective-permute-start | bytes 49160 | tf_op jit(solution)/shard_map/while/body/eval_jaxpr/ppermute | solution.py:21
  207.9 8.2 %collective-permute-start.2 = (f32[80,8]{1,0:T(8,128)S(1)}, f32[80,8]{1,0:T(8,128)S(1)}, u32[]{:S(2)}, u32[]{:S(2)}) collective-permute-start(f32[80,8]{1,0:T(8,128)S(1)} %get-tuple-element.129), channel_id=1, source_target_pairs={{1,0},{2,1},{3,2},{4,3},{5,4},{6,5},{7,6},{8,7},{9,8},{10,9},{11,1... | collective-permute-start | bytes 7688 | tf_op jit(solution)/shard_map/while/body/eval_jaxpr/ppermute | solution.py:21
  209.8 7.4 %collective-permute-start.3 = (f32[80,8]{1,0:T(8,128)S(1)}, f32[80,8]{1,0:T(8,128)S(1)}, u32[]{:S(2)}, u32[]{:S(2)}) collective-permute-start(f32[80,8]{1,0:T(8,128)S(1)} %get-tuple-element.130), channel_id=1, source_target_pairs={{0,1},{1,2},{2,3},{3,4},{4,5},{5,6},{6,7},{7,8},{8,9},{9,10},{10,1... | collective-permute-start | bytes 7688 | tf_op jit(solution)/shard_map/while/body/eval_jaxpr/ppermute | solution.py:20
  223.5 8.0 %collective-permute-start = (f32[8,512]{1,0:T(8,128)S(1)}, f32[8,512]{1,0:T(8,128)S(1)}, u32[]{:S(2)}, u32[]{:S(2)}) collective-permute-start(f32[8,512]{1,0:T(8,128)S(1)} %get-tuple-element.127), channel_id=1, source_target_pairs={{0,16},{16,32},{32,48},{48,64},{64,80},{80,96},{96,112},{112,128},... | collective-permute-start | bytes 49160 | tf_op jit(solution)/shard_map/while/body/eval_jaxpr/ppermute | solution.py:20
  225.4 6.9 %collective-permute-start.1 = (f32[8,512]{1,0:T(8,128)S(1)}, f32[8,512]{1,0:T(8,128)S(1)}, u32[]{:S(2)}, u32[]{:S(2)}) collective-permute-start(f32[8,512]{1,0:T(8,128)S(1)} %get-tuple-element.128), channel_id=1, source_target_pairs={{16,0},{32,16},{48,32},{64,48},{80,64},{96,80},{112,96},{128,112},... | collective-permute-start | bytes 49160 | tf_op jit(solution)/shard_map/while/body/eval_jaxpr/ppermute | solution.py:21
  232.3 8.2 %collective-permute-start.2 = (f32[80,8]{1,0:T(8,128)S(1)}, f32[80,8]{1,0:T(8,128)S(1)}, u32[]{:S(2)}, u32[]{:S(2)}) collective-permute-start(f32[80,8]{1,0:T(8,128)S(1)} %get-tuple-element.129), channel_id=1, source_target_pairs={{1,0},{2,1},{3,2},{4,3},{5,4},{6,5},{7,6},{8,7},{9,8},{10,9},{11,1... | collective-permute-start | bytes 7688 | tf_op jit(solution)/shard_map/while/body/eval_jaxpr/ppermute | solution.py:21
  234.3 7.4 %collective-permute-start.3 = (f32[80,8]{1,0:T(8,128)S(1)}, f32[80,8]{1,0:T(8,128)S(1)}, u32[]{:S(2)}, u32[]{:S(2)}) collective-permute-start(f32[80,8]{1,0:T(8,128)S(1)} %get-tuple-element.130), channel_id=1, source_target_pairs={{0,1},{1,2},{2,3},{3,4},{4,5},{5,6},{6,7},{7,8},{8,9},{9,10},{10,1... | collective-permute-start | bytes 7688 | tf_op jit(solution)/shard_map/while/body/eval_jaxpr/ppermute | solution.py:20
  247.9 8.0 %collective-permute-start = (f32[8,512]{1,0:T(8,128)S(1)}, f32[8,512]{1,0:T(8,128)S(1)}, u32[]{:S(2)}, u32[]{:S(2)}) collective-permute-start(f32[8,512]{1,0:T(8,128)S(1)} %get-tuple-element.127), channel_id=1, source_target_pairs={{0,16},{16,32},{32,48},{48,64},{64,80},{80,96},{96,112},{112,128},... | collective-permute-start | bytes 49160 | tf_op jit(solution)/shard_map/while/body/eval_jaxpr/ppermute | solution.py:20
  249.9 6.9 %collective-permute-start.1 = (f32[8,512]{1,0:T(8,128)S(1)}, f32[8,512]{1,0:T(8,128)S(1)}, u32[]{:S(2)}, u32[]{:S(2)}) collective-permute-start(f32[8,512]{1,0:T(8,128)S(1)} %get-tuple-element.128), channel_id=1, source_target_pairs={{16,0},{32,16},{48,32},{64,48},{80,64},{96,80},{112,96},{128,112},... | collective-permute-start | bytes 49160 | tf_op jit(solution)/shard_map/while/body/eval_jaxpr/ppermute | solution.py:21
  256.8 8.2 %collective-permute-start.2 = (f32[80,8]{1,0:T(8,128)S(1)}, f32[80,8]{1,0:T(8,128)S(1)}, u32[]{:S(2)}, u32[]{:S(2)}) collective-permute-start(f32[80,8]{1,0:T(8,128)S(1)} %get-tuple-element.129), channel_id=1, source_target_pairs={{1,0},{2,1},{3,2},{4,3},{5,4},{6,5},{7,6},{8,7},{9,8},{10,9},{11,1... | collective-permute-start | bytes 7688 | tf_op jit(solution)/shard_map/while/body/eval_jaxpr/ppermute | solution.py:21
  258.7 7.4 %collective-permute-start.3 = (f32[80,8]{1,0:T(8,128)S(1)}, f32[80,8]{1,0:T(8,128)S(1)}, u32[]{:S(2)}, u32[]{:S(2)}) collective-permute-start(f32[80,8]{1,0:T(8,128)S(1)} %get-tuple-element.130), channel_id=1, source_target_pairs={{0,1},{1,2},{2,3},{3,4},{4,5},{5,6},{6,7},{7,8},{8,9},{9,10},{10,1... | collective-permute-start | bytes 7688 | tf_op jit(solution)/shard_map/while/body/eval_jaxpr/ppermute | solution.py:20
  272.4 8.0 %collective-permute-start = (f32[8,512]{1,0:T(8,128)S(1)}, f32[8,512]{1,0:T(8,128)S(1)}, u32[]{:S(2)}, u32[]{:S(2)}) collective-permute-start(f32[8,512]{1,0:T(8,128)S(1)} %get-tuple-element.127), channel_id=1, source_target_pairs={{0,16},{16,32},{32,48},{48,64},{64,80},{80,96},{96,112},{112,128},... | collective-permute-start | bytes 49160 | tf_op jit(solution)/shard_map/while/body/eval_jaxpr/ppermute | solution.py:20
  274.3 6.9 %collective-permute-start.1 = (f32[8,512]{1,0:T(8,128)S(1)}, f32[8,512]{1,0:T(8,128)S(1)}, u32[]{:S(2)}, u32[]{:S(2)}) collective-permute-start(f32[8,512]{1,0:T(8,128)S(1)} %get-tuple-element.128), channel_id=1, source_target_pairs={{16,0},{32,16},{48,32},{64,48},{80,64},{96,80},{112,96},{128,112},... | collective-permute-start | bytes 49160 | tf_op jit(solution)/shard_map/while/body/eval_jaxpr/ppermute | solution.py:21
  281.3 8.2 %collective-permute-start.2 = (f32[80,8]{1,0:T(8,128)S(1)}, f32[80,8]{1,0:T(8,128)S(1)}, u32[]{:S(2)}, u32[]{:S(2)}) collective-permute-start(f32[80,8]{1,0:T(8,128)S(1)} %get-tuple-element.129), channel_id=1, source_target_pairs={{1,0},{2,1},{3,2},{4,3},{5,4},{6,5},{7,6},{8,7},{9,8},{10,9},{11,1... | collective-permute-start | bytes 7688 | tf_op jit(solution)/shard_map/while/body/eval_jaxpr/ppermute | solution.py:21
  283.2 7.4 %collective-permute-start.3 = (f32[80,8]{1,0:T(8,128)S(1)}, f32[80,8]{1,0:T(8,128)S(1)}, u32[]{:S(2)}, u32[]{:S(2)}) collective-permute-start(f32[80,8]{1,0:T(8,128)S(1)} %get-tuple-element.130), channel_id=1, source_target_pairs={{0,1},{1,2},{2,3},{3,4},{4,5},{5,6},{6,7},{7,8},{8,9},{9,10},{10,1... | collective-permute-start | bytes 7688 | tf_op jit(solution)/shard_map/while/body/eval_jaxpr/ppermute | solution.py:20
  296.9 0.7 copy-start
where the time goes:
time: 301 us; the launch traced here: 298 us
  starting transfers between devices  214 us (71%)
  other arithmetic  54.4 us (18%)
  waiting for transfers between devices  25.6 us (9%)
    ppermute x28, starting transfers between devices, extended(): after = lax.ppermute(initial, axis, down)  108 us
    ppermute x28, starting transfers between devices, extended(): before = lax.ppermute(last, axis, up)  106 us
    select_n x64, other arithmetic, group_pass(): sent = jnp.where(route_here > 0, current, jnp.float32(0.0))  45.4 us
    ppermute x28, waiting for transfers between devices, extended(): after = lax.ppermute(initial, axis, down)  16.2 us
    ppermute x28, waiting for transfers between devices, extended(): before = lax.ppermute(last, axis, up)  9.45 us
  transfers between devices with their start and end apart: 56, of which 20 were waited for; matrix products, arithmetic and copies ran while one was open for 0% of the time, Pallas kernels for 0%

commit v1 on v0

v1 whole, which is shorter than its diff:
```python
import functools

import jax
import jax.numpy as jnp
from jax import lax
from jax.experimental import pallas as pl
from jax.experimental.pallas import tpu as pltpu
from jax.sharding import PartitionSpec as P

SUBSTEPS = 3
PASSES = 64
MARGIN = 32
NEAR = 8
LANES = 128
MESH = pl.DeviceIdType.MESH
OFFSETS = ((0, 1), (1, 1), (1, 0), (1, -1), (0, -1), (-1, -1), (-1, 0), (-1, 1))
SIDES = ((-1, 0), (1, 0), (0, -1), (0, 1), (-1, -1), (-1, 1), (1, -1), (1, 1))


def kernel(
    rows, cols, nrow, ncol,
    depth, rainfall, conveyance, flow_dir, outlet, new_depth, discharge,
    raw, raw_side, flow, out_of, route, route_side, level, level_side, sent, masks, acc, far,
    in_sem, out_sem, raw_ssem, raw_rsem, route_ssem, route_rsem, level_ssem, level_rsem, far_ssem, far_rsem,
):
    strips = cols // LANES
    total = strips + 1
    top = MARGIN + 8
    end = top + rows
    me_r, me_c = lax.axis_index("row"), lax.axis_index("col")
    lane = lax.broadcasted_iota(jnp.int32, (8, LANES), 1)
    zero = jnp.zeros((8, LANES), jnp.float32)

    def present(dr, dc):
        r, c = me_r + dr, me_c + dc
        return (r >= 0) & (r < nrow) & (c >= 0) & (c < ncol)

    loads = []
    for a, (source, target) in enumerate((
        (flow_dir, flow), (outlet, out_of), (depth, raw.at[0]), (rainfall, raw.at[1]), (conveyance, raw.at[2]),
    )):
        for w in range(strips):
            rows_at = pl.ds(0, rows) if a < 2 else pl.ds(top, rows)
            loads.append(pltpu.make_async_copy(
                source.at[:, pl.ds(w * LANES, LANES)], target.at[w, rows_at, :], in_sem.at[a, w]))
    for load in loads:
        load.start()

    def clear(ref, first, last):
        for r in range(first, last, 8):
            ref[pl.ds(r, 8), :] = zero

    for w in range(strips):
        for a in range(3):
            clear(raw.at[a, w], top - NEAR, top)
            clear(raw.at[a, w], end, end + NEAR)
        for ref in (route, level):
            clear(ref.at[w], top - MARGIN, top)
            clear(ref.at[w], end, end + MARGIN)
    for side in range(2):
        for a in range(3):
            clear(raw_side.at[side, a], top - NEAR, end + NEAR)
        for ref in (route_side, level_side):
            clear(ref.at[side], top - MARGIN, end + MARGIN)
        for w in range(total):
            clear(far.at[side, w], 0, MARGIN)

    barrier = pltpu.get_barrier_semaphore()
    neighbours = jnp.int32(0)
    for dr, dc in SIDES:
        here = present(dr, dc)
        neighbours = neighbours + here.astype(jnp.int32)

        @pl.when(here)
        def _():
            pl.semaphore_signal(barrier, inc=1, device_id=(me_r + dr, me_c + dc), device_id_type=MESH)

    def copies(main, side, reach, ssem, rsem):
        made = []
        for d, (dr, dc) in enumerate(SIDES):
            if dr == 0:
                source, target = pl.ds(top, rows), pl.ds(top, rows)
            elif dr < 0:
                source, target = pl.ds(top, reach), pl.ds(end, reach)
            else:
                source, target = pl.ds(end - reach, reach), pl.ds(top - reach, reach)
            if dc == 0:
                src, dst = main(None, source), main(None, target)
            elif dc < 0:
                src, dst = main(0, source), side(1, target)
            else:
                src, dst = main(strips - 1, source), side(0, target)
            made.append(pltpu.make_async_remote_copy(
                src_ref=src, dst_ref=dst, send_sem=ssem.at[d], recv_sem=rsem.at[d],
                device_id=(me_r + dr, me_c + dc), device_id_type=MESH))
        return made

    def on_each(made, act, flip):
        for copy, (dr, dc) in zip(made, SIDES):
            @pl.when(present(-dr, -dc) if flip else present(dr, dc))
            def _():
                act(copy)

    def start_all(made):
        on_each(made, lambda copy: copy.start(), False)

    def arrive_all(made):
        on_each(made, lambda copy: copy.wait_recv(), True)

    def leave_all(made):
        on_each(made, lambda copy: copy.wait_send(), False)

    raw_copies = copies(
        lambda w, at: raw.at[:, pl.ds(0, strips), at, :] if w is None else raw.at[:, w, at, :],
        lambda s, at: raw_side.at[s, :, at, :], NEAR, raw_ssem, raw_rsem)
    route_copies = copies(
        lambda w, at: route.at[pl.ds(0, strips), at, :] if w is None else route.at[w, at, :],
        lambda s, at: route_side.at[s, at, :], MARGIN, route_ssem, route_rsem)
    level_copies = copies(
        lambda w, at: level.at[pl.ds(0, strips), at, :] if w is None else level.at[w, at, :],
        lambda s, at: level_side.at[s, at, :], MARGIN, level_ssem, level_rsem)

    for load in loads:
        load.wait()
    for w in range(strips):
        for r in range(0, rows, 8):
            at, here = pl.ds(r, 8), pl.ds(top + r, 8)
            code = flow[w, at, :]
            route[w, here, :] = jnp.where(out_of[w, at, :] == 1, 0, code + 1).astype(jnp.float32)
            length = jnp.where(code % 2 == 1, jnp.float32(0.70710678), jnp.float32(1.0))
            raw[2, w, here, :] = raw[2, w, here, :] * length

    pl.semaphore_wait(barrier, neighbours)
    start_all(raw_copies)
    start_all(route_copies)

    def merge(main, side, first, last):
        for r in range(first, last, 8):
            at = pl.ds(r, 8)
            main[strips, at, :] = jnp.where(lane < LANES // 2, side[1, at, :], side[0, at, :])

    arrive_all(raw_copies)
    arrive_all(route_copies)
    for a in range(3):
        merge(raw.at[a], raw_side.at[:, a], top - NEAR, end + NEAR)
    merge(route, route_side, top - MARGIN, end + MARGIN)

    def make_masks(first, last):
        for w in range(total):
            for r in range(first, last, 8):
                near = {di: route[w, pl.ds(r - di, 8), :] for di in (-1, 0, 1)}
                for k, (di, dj) in enumerate(OFFSETS):
                    masks[k, w, pl.ds(r, 8), :] = jnp.where(
                        near[di] == jnp.float32(k + 1), jnp.float32(1.0), jnp.float32(0.0))

    def inflow(source, base, r):
        east, west, still = [], [], []
        here = pl.ds(r, 8)
        for w in range(total):
            x = {di: source[w, pl.ds(r - di, 8), :] for di in (-1, 0, 1)}
            term = [masks[k, w, here, :] * x[di] for k, (di, _) in enumerate(OFFSETS)]
            east.append(term[0] + term[1] + term[7])
            west.append(term[3] + term[4] + term[5])
            still.append(base(w, here) + term[2] + term[6])
        east = [pltpu.roll(x, 1, 1) for x in east]
        west = [pltpu.roll(x, LANES - 1, 1) for x in west]
        return [
            still[w]
            + jnp.where(lane == 0, east[w - 1], east[w])
            + jnp.where(lane == LANES - 1, west[(w + 1) % total], west[w])
            for w in range(total)
        ]

    make_masks(top - NEAR, end + NEAR)
    for step in range(SUBSTEPS):
        held = raw.at[0] if step == 0 else acc.at[0]
        for w in range(total):
            for r in range(top - NEAR, end + NEAR, 8):
                at = pl.ds(r, 8)
                h = held[w, at, :]
                factor = raw[2, w, at, :] * jnp.exp(jnp.log(h) * jnp.float32(2.0 / 3.0))
                out = h * (factor / (1.0 + factor))
                sent[w, at, :] = out
                acc[0, w, at, :] = h + raw[1, w, at, :] - out
        target = acc.at[0] if step < SUBSTEPS - 1 else level
        for r in range(top - NEAR, end + NEAR, 8):
            if step == SUBSTEPS - 1 and not top <= r < end:
                continue
            new = inflow(sent, lambda w, at: acc[0, w, at, :], r)
            for w in range(total if step < SUBSTEPS - 1 else strips):
                target[w, pl.ds(r, 8), :] = new[w]

    start_all(level_copies)
    stores = [
        pltpu.make_async_copy(
            level.at[w, pl.ds(top, rows), :], new_depth.at[:, pl.ds(w * LANES, LANES)], out_sem.at[0, w])
        for w in range(strips)
    ]
    for store in stores:
        store.start()
    make_masks(top - MARGIN, top - NEAR)
    make_masks(end + NEAR, end + MARGIN)
    arrive_all(level_copies)
    merge(level, level_side, top - MARGIN, end + MARGIN)

    def one_pass(source, target, first, last):
        for r in range(first, last, 8):
            new = inflow(source, lambda w, at: level[w, at, :], r)
            for w in range(total):
                target[w, pl.ds(r, 8), :] = new[w]

    def segment(source):
        one_pass(source, acc.at[1], top - MARGIN, end + MARGIN)
        one_pass(acc.at[1], acc.at[0], top - MARGIN, end + MARGIN)
        for g in range(0, MARGIN, 8):
            def pair(_, carry):
                one_pass(acc.at[0], acc.at[1], top - MARGIN + g, end + MARGIN - g)
                one_pass(acc.at[1], acc.at[0], top - MARGIN + g, end + MARGIN - g)
                return carry

            lax.fori_loop(1 if g == 0 else 0, 4, pair, 0)

    segment(level)
    for seg in range(1, PASSES // MARGIN):
        up = pltpu.make_async_remote_copy(
            src_ref=acc.at[0, :, pl.ds(top, MARGIN), :], dst_ref=far.at[1], send_sem=far_ssem.at[seg, 0],
            recv_sem=far_rsem.at[seg, 0], device_id=(me_r - 1, me_c), device_id_type=MESH)
        down = pltpu.make_async_remote_copy(
            src_ref=acc.at[0, :, pl.ds(end - MARGIN, MARGIN), :], dst_ref=far.at[0], send_sem=far_ssem.at[seg, 1],
            recv_sem=far_rsem.at[seg, 1], device_id=(me_r + 1, me_c), device_id_type=MESH)
        has_up, has_down = present(-1, 0), present(1, 0)
        pl.when(has_up)(lambda: up.start())
        pl.when(has_down)(lambda: down.start())
        pl.when(has_down)(lambda: up.wait_recv())
        pl.when(has_up)(lambda: down.wait_recv())
        pl.when(has_up)(lambda: up.wait_send())
        pl.when(has_down)(lambda: down.wait_send())
        for w in range(total):
            for r in range(0, MARGIN, 8):
                acc[0, w, pl.ds(top - MARGIN + r, 8), :] = far[0, w, pl.ds(r, 8), :]
                acc[0, w, pl.ds(end + r, 8), :] = far[1, w, pl.ds(r, 8), :]
        segment(acc.at[0])

    for w in range(strips):
        for r in range(0, rows, 8):
            sent[w, pl.ds(top + r, 8), :] = jnp.log(1.0 + acc[0, w, pl.ds(top + r, 8), :])
    ends = [
        pltpu.make_async_copy(
            sent.at[w, pl.ds(top, rows), :], discharge.at[:, pl.ds(w * LANES, LANES)], out_sem.at[1, w])
        for w in range(strips)
    ]
    for store in ends:
        store.start()
    leave_all(raw_copies)
    leave_all(route_copies)
    leave_all(level_copies)
    for store in stores + ends:
        store.wait()


def solution(mesh):
    nrow, ncol = mesh.shape["row"], mesh.shape["col"]

    def on_device(depth, rainfall, conveyance, flow_dir, outlet):
        rows, cols = depth.shape
        strips = cols // LANES
        total = strips + 1
        high = rows + 2 * MARGIN + 16
        f32 = functools.partial(pltpu.VMEM, dtype=jnp.float32)
        dma = pltpu.SemaphoreType.DMA
        segments = PASSES // MARGIN
        return tuple(pl.pallas_call(
            functools.partial(kernel, rows, cols, nrow, ncol),
            out_shape=[jax.ShapeDtypeStruct((rows, cols), jnp.float32)] * 2,
            in_specs=[pl.BlockSpec(memory_space=pl.ANY)] * 5,
            out_specs=[pl.BlockSpec(memory_space=pl.ANY)] * 2,
            scratch_shapes=[
                f32((3, total, high, LANES)),
                f32((2, 3, high, LANES)),
                pltpu.VMEM((strips, rows, LANES), jnp.int32),
                pltpu.VMEM((strips, rows, LANES), jnp.int32),
                f32((total, high, LANES)),
                f32((2, high, LANES)),
                f32((total, high, LANES)),
                f32((2, high, LANES)),
                f32((total, high, LANES)),
                f32((8, total, high, LANES)),
                f32((2, total, high, LANES)),
                f32((2, total, MARGIN, LANES)),
                dma((5, strips)),
                dma((2, strips)),
                dma((8,)), dma((8,)), dma((8,)), dma((8,)), dma((8,)), dma((8,)),
                dma((segments, 2)), dma((segments, 2)),
            ],
            compiler_params=pltpu.CompilerParams(collective_id=0, has_side_effects=True),
            name="overland",
        )(depth, rainfall, conveyance, flow_dir, outlet))

    placed = P("row", "col")
    return jax.shard_map(
        on_device, mesh=mesh, in_specs=(placed,) * 5, out_specs=(placed, placed), check_vma=False)
```

time: 301 us -> 39.9 us (0.13); the launches traced: 298 us -> 39.7 us
  starting transfers between devices: 214 us -> 0 us
  other arithmetic: 54.4 us -> 0 us
  Pallas kernels: 0 us -> 36.8 us
  waiting for transfers between devices: 25.6 us -> 0 us
    ppermute x56 -> x0, starting transfers between devices: 214 us -> none  [the longest x28 108 us: extended(): after = lax.ppermute(initial, axis, down)]
    select_n x67 -> x0, other arithmetic: 48.1 us -> none  [the longest x64 45.4 us: group_pass(): sent = jnp.where(route_here > 0, current, jnp.float32(0.0))]
    pallas_call x0 -> x1, Pallas kernels: none -> 36.8 us  [on_device(): pl.pallas_call(functools.partial(kernel, rows, cols, nrow, ncol), out_sha...]
    ppermute x56 -> x0, waiting for transfers between devices: 25.6 us -> none  [the longest x28 16.2 us: extended(): after = lax.ppermute(initial, axis, down)]
    add x9 -> x0, other arithmetic: 4.46 us -> none  [the longest x8 4.06 us: group_pass(): current = level_here + padded_inflow(sent, route_here)]
  transfers between devices with their start and end apart: 56 -> 0, of which waited for: 20 -> 0; matrix products, arithmetic and copies ran while one was open for 0% -> 0% of each run, Pallas kernels for 0% -> 0%
where the time goes in v1:
time: 39.9 us; the launch traced here: 39.7 us
  Pallas kernels  36.8 us (92%)
  local copies, waits for them, and re-layouts  2.26 us (6%)
  between operations  0.65 us (2%)
    pallas_call x1, Pallas kernels, on_device(): pl.pallas_call(functools.partial(kernel, rows, cols, nrow, ncol), out_sha...  36.8 us
    unnamed x4, local copies, waits for them, and re-layouts  2.26 us

profile of v1, /device:TPU:121, one launch (start us, length us, event | category | flops | bytes accessed | tf_op | source)
XLA Modules:
  0.0 39.7 jit_solution(2769089730063243819)
XLA Ops:
  0.6 36.8 %overland.1 = (f32[64,512]{1,0:T(8,128)}, f32[64,512]{1,0:T(8,128)}) custom-call(f32[64,512]{1,0:T(8,128)} %depth.1, f32[64,512]{1,0:T(8,128)} %rainfall.1, f32[64,512]{1,0:T(8,128)} %conveyance.1, s32[64,512]{1,0:T(8,128)} %flow_dir.1, s32[64,512]{1,0:T(8,128)} %outlet.1), custom_call_target="tpu_custom_call" | custom-call | tf_op jit(solution)/shard_map/overland/pallas_call | solution.py:272
  37.4 0.0 copy-start
  37.4 1.6 %copy.9 = f32[64,512]{1,0:T(8,128)} copy(f32[64,512]{1,0:T(8,128)} %get-tuple-element.4) | data formatting | bytes 262144
  39.0 0.0 copy-done
  39.0 0.7 %copy.10 = f32[64,512]{1,0:T(8,128)} copy(f32[64,512]{1,0:T(8,128)S(1)} %copy-done) | data formatting | bytes 262144
Async XLA Ops:
  37.4 1.6 %copy-start = (f32[64,512]{1,0:T(8,128)S(1)}, f32[64,512]{1,0:T(8,128)}, u32[]{:S(2)}) copy-start(f32[64,512]{1,0:T(8,128)} %get-tuple-element.5) | copy-start | bytes 393220

commit v2 on v1

v2 whole, which is shorter than its diff:
```python
import functools

import jax
import jax.numpy as jnp
from jax import lax
from jax.experimental import pallas as pl
from jax.experimental.pallas import tpu as pltpu
from jax.sharding import PartitionSpec as P

SUBSTEPS = 3
PASSES = 64
MARGIN = 32
INNER = 16
LANES = 128
NEAR = 4
MESH = pl.DeviceIdType.MESH
OFFSETS = ((0, 1), (1, 1), (1, 0), (1, -1), (0, -1), (-1, -1), (-1, 0), (-1, 1))
SIDES = ((-1, 0), (1, 0), (0, -1), (0, 1), (-1, -1), (-1, 1), (1, -1), (1, 1))
VERTICAL = ((-1, 0), (1, 0))


def starts(first, last):
    made = list(range(first, last - 7, 8))
    if made[-1] + 8 < last:
        made.append(last - 8)
    return made


def kernel(
    rows, cols, nrow, ncol,
    depth, rainfall, conveyance, flow_dir, outlet, new_depth, discharge,
    near, flow, out_of, pack, landed, route, level, sent, rest, masks, state, far, final,
    in_sem, out_sem, near_ssem, near_rsem, route_ssem, route_rsem, far_ssem, far_rsem,
):
    strips = cols // LANES
    mid, left, right = strips, strips + 1, strips + 2
    inner_order = list(range(strips)) + [mid]
    near_order = [left] + list(range(strips)) + [right]
    top = MARGIN + 8
    end = top + rows
    base = 16
    me_r, me_c = lax.axis_index("row"), lax.axis_index("col")
    lane = lax.broadcasted_iota(jnp.int32, (8, LANES), 1)
    zero = jnp.zeros((8, LANES), jnp.float32)
    own = pl.ds(base, rows)

    def present(dr, dc):
        r, c = me_r + dr, me_c + dc
        return (r >= 0) & (r < nrow) & (c >= 0) & (c < ncol)

    loads = []
    for a, (source, target) in enumerate((
        (flow_dir, flow), (outlet, out_of), (depth, near.at[0]), (rainfall, near.at[1]), (conveyance, near.at[2]),
    )):
        for w in range(strips):
            loads.append(pltpu.make_async_copy(
                source.at[:, pl.ds(w * LANES, LANES)],
                target.at[w, pl.ds(0, rows) if a < 2 else own, :], in_sem.at[a, w]))
    for load in loads:
        load.start()

    def clear(ref, first, last):
        for r in range(first, last, 8):
            ref[pl.ds(r, 8), :] = zero

    for half in range(2):
        for w in near_order:
            clear(landed.at[half, w], 8, 8 + 4 * NEAR)
        for seg in range(PASSES // MARGIN):
            for w in inner_order:
                clear(far.at[seg, half, w], 0, MARGIN)
    for a in range(4):
        for w in (left, right):
            clear(near.at[a, w], base, base + rows)
    for w in inner_order:
        clear(route.at[w], top - MARGIN, top)
        clear(route.at[w], end, end + MARGIN)

    barrier = pltpu.get_barrier_semaphore()
    neighbours = jnp.int32(0)
    for dr, dc in SIDES:
        here = present(dr, dc)
        neighbours = neighbours + here.astype(jnp.int32)

        @pl.when(here)
        def _():
            pl.semaphore_signal(barrier, inc=1, device_id=(me_r + dr, me_c + dc), device_id_type=MESH)

    def remote(side, src, dst, ssem, rsem):
        return side, pltpu.make_async_remote_copy(
            src_ref=src, dst_ref=dst, send_sem=ssem, recv_sem=rsem,
            device_id=(me_r + side[0], me_c + side[1]), device_id_type=MESH)

    def start_all(made):
        for (dr, dc), copy in made:
            pl.when(present(dr, dc))(lambda: copy.start())

    def arrive_all(made):
        for (dr, dc), copy in made:
            pl.when(present(-dr, -dc))(lambda: copy.wait_recv())

    def leave_all(made):
        for (dr, dc), copy in made:
            pl.when(present(dr, dc))(lambda: copy.wait_send())

    near_copies = []
    for d, (dr, dc) in enumerate(SIDES):
        if dr == 0:
            src = near.at[:, 0 if dc < 0 else strips - 1, own, :]
            dst = near.at[:, right if dc < 0 else left, own, :]
        else:
            half, at = (0 if dr < 0 else 1), pl.ds(8, 4 * NEAR)
            if dc == 0:
                src, dst = pack.at[half, :, at, :], landed.at[1 - half, pl.ds(0, strips), at, :]
            else:
                src = pack.at[half, 0 if dc < 0 else strips - 1, at, :]
                dst = landed.at[1 - half, right if dc < 0 else left, at, :]
        near_copies.append(remote((dr, dc), src, dst, near_ssem.at[d], near_rsem.at[d]))

    edge = {-1: (pl.ds(top, MARGIN), pl.ds(end, MARGIN)), 1: (pl.ds(end - MARGIN, MARGIN), pl.ds(top - MARGIN, MARGIN))}
    route_copies, route_mid_copies = [], []
    for d, (dr, dc) in enumerate(VERTICAL):
        source, target = edge[dr]
        route_copies.append(remote(
            (dr, dc), route.at[pl.ds(0, strips), source, :], route.at[pl.ds(0, strips), target, :],
            route_ssem.at[0, d], route_rsem.at[0, d]))
        route_mid_copies.append(remote(
            (dr, dc), route.at[mid, source, :], route.at[mid, target, :], route_ssem.at[1, d], route_rsem.at[1, d]))

    def far_copies(source, seg):
        return [
            remote((dr, dc), source.at[:, edge[dr][0], :], far.at[seg, 1 - d], far_ssem.at[seg, d], far_rsem.at[seg, d])
            for d, (dr, dc) in enumerate(VERTICAL)
        ]

    for load in loads:
        load.wait()
    for w in range(strips):
        for r in range(0, rows, 8):
            at, here = pl.ds(r, 8), pl.ds(base + r, 8)
            code = flow[w, at, :]
            kind = jnp.where(out_of[w, at, :] == 1, 0, code + 1).astype(jnp.float32)
            near[3, w, here, :] = kind
            route[w, pl.ds(top + r, 8), :] = kind
            length = jnp.where(code % 2 == 1, jnp.float32(0.70710678), jnp.float32(1.0))
            near[2, w, here, :] = near[2, w, here, :] * length
        for a in range(4):
            pack[0, w, pl.ds(8 + NEAR * a, 8), :] = near[a, w, pl.ds(base, 8), :]
        for a in reversed(range(4)):
            pack[1, w, pl.ds(8 + NEAR * (a - 1), 8), :] = near[a, w, pl.ds(base + rows - 8, 8), :]

    pl.semaphore_wait(barrier, neighbours)
    start_all(near_copies)
    start_all(route_copies)

    arrive_all(near_copies)
    for r in range(0, rows, 8):
        here = pl.ds(base + r, 8)
        route[mid, pl.ds(top + r, 8), :] = jnp.where(lane < LANES // 2, near[3, right, here, :], near[3, left, here, :])
    start_all(route_mid_copies)
    for w in near_order:
        for a in range(4):
            near[a, w, pl.ds(base - 8, 8), :] = landed[0, w, pl.ds(8 + NEAR * (a - 1), 8), :]
            near[a, w, pl.ds(base + rows, 8), :] = landed[1, w, pl.ds(8 + NEAR * a, 8), :]

    def make_masks(codes, shift, w, r):
        around = {di: codes[w, pl.ds(r + shift - di, 8), :] for di in (-1, 0, 1)}
        for k, (di, dj) in enumerate(OFFSETS):
            masks[k, w, pl.ds(r, 8), :] = jnp.where(
                around[di] == jnp.float32(k + 1), jnp.float32(1.0), jnp.float32(0.0))

    def inflow(source, shift, order, held, r):
        east, west, still = [], [], []
        count = len(order)
        for w in order:
            x = {di: source[w, pl.ds(r + shift - di, 8), :] for di in (-1, 0, 1)}
            term = [masks[k, w, pl.ds(r, 8), :] * x[di] for k, (di, _) in enumerate(OFFSETS)]
            east.append(term[0] + term[1] + term[7])
            west.append(term[3] + term[4] + term[5])
            still.append(held[w, pl.ds(r + shift, 8), :] + term[2] + term[6])
        east = [pltpu.roll(x, 1, 1) for x in east]
        west = [pltpu.roll(x, LANES - 1, 1) for x in west]
        return [
            still[i]
            + jnp.where(lane == 0, east[i - 1], east[i])
            + jnp.where(lane == LANES - 1, west[(i + 1) % count], west[i])
            for i in range(count)
        ]

    for w in near_order:
        for r in starts(top - NEAR, end + NEAR):
            make_masks(near.at[3], base - top, w, r)
    for r in starts(top + 1, end - 1):
        make_masks(route, 0, mid, r)
    for step in range(SUBSTEPS):
        held = near.at[0] if step == 0 else final
        for w in near_order:
            for r in starts(base - NEAR, base + rows + NEAR):
                at = pl.ds(r, 8)
                h = held[w, at, :]
                factor = near[2, w, at, :] * jnp.exp(jnp.log(h) * jnp.float32(2.0 / 3.0))
                out = h * (factor / (1.0 + factor))
                sent[w, at, :] = out
                rest[w, at, :] = h + near[1, w, at, :] - out
        if step < SUBSTEPS - 1:
            for r in starts(top - NEAR, end + NEAR):
                new = inflow(sent, base - top, near_order, rest, r)
                for w, value in zip(near_order, new):
                    final[w, pl.ds(r + base - top, 8), :] = value
    for r in range(top, end, 8):
        new = inflow(sent, base - top, near_order, rest, r)
        for w, value in enumerate(new[1:-1] + [jnp.where(lane < LANES // 2, new[-1], new[0])]):
            level[w, pl.ds(r, 8), :] = value
            state[0, w, pl.ds(r, 8), :] = value

    start_all(far_copies(level, 0))
    stores = [
        pltpu.make_async_copy(
            level.at[w, pl.ds(top, rows), :], new_depth.at[:, pl.ds(w * LANES, LANES)], out_sem.at[0, w])
        for w in range(strips)
    ]
    for store in stores:
        store.start()

    lanes = lax.broadcasted_iota(jnp.int32, (strips + 1, 8, LANES), 2)

    def one_pass(p, blocks):
        for r in blocks:
            x = {di: state[p, :, pl.ds(r - di, 8), :] for di in (-1, 0, 1)}
            term = [masks[k, pl.ds(0, strips + 1), pl.ds(r, 8), :] * x[di] for k, (di, _) in enumerate(OFFSETS)]
            east = pltpu.roll(term[0] + term[1] + term[7], 1, 2)
            west = pltpu.roll(term[3] + term[4] + term[5], LANES - 1, 2)
            still = level[:, pl.ds(r, 8), :] + term[2] + term[6]
            before = jnp.concatenate([east[strips:], east[:strips]], axis=0)
            after = jnp.concatenate([west[1:], west[:1]], axis=0)
            value = still + jnp.where(lanes == 0, before, east) + jnp.where(lanes == LANES - 1, after, west)
            state[p + 1, :, pl.ds(r, 8), :] = value
            if p == MARGIN - 1:
                state[0, :, pl.ds(r, 8), :] = value

    def segment(seg, carry):
        for p in range(INNER):
            one_pass(p, starts(top + p + 1, end - p - 1))

        @pl.when(seg == 0)
        def _():
            arrive_all(route_copies)
            arrive_all(route_mid_copies)
            for w in inner_order:
                for r in range(top - MARGIN, top + (8 if w == mid else 0), 8):
                    make_masks(route, 0, w, r)
                for r in range(end - (8 if w == mid else 0), end + MARGIN, 8):
                    make_masks(route, 0, w, r)

        arrive_all(far_copies(level, seg))
        leave_all(far_copies(level, seg))
        for w in inner_order:
            for r in range(0, MARGIN, 8):
                state[0, w, pl.ds(top - MARGIN + r, 8), :] = far[seg, 0, w, pl.ds(r, 8), :]
                state[0, w, pl.ds(end + r, 8), :] = far[seg, 1, w, pl.ds(r, 8), :]

        @pl.when(seg == 0)
        def _():
            for w in inner_order:
                for r in range(0, MARGIN, 8):
                    level[w, pl.ds(top - MARGIN + r, 8), :] = far[0, 0, w, pl.ds(r, 8), :]
                    level[w, pl.ds(end + r, 8), :] = far[0, 1, w, pl.ds(r, 8), :]

        for p in range(MARGIN):
            above, below = top - MARGIN + p + 1, end + MARGIN - p - 1
            if p < INNER:
                one_pass(p, starts(above, above + MARGIN) + starts(below - MARGIN, below))
            else:
                one_pass(p, starts(above, below))

        @pl.when(seg == 0)
        def _():
            start_all(far_copies(state.at[MARGIN], 1))

        return carry

    lax.fori_loop(0, PASSES // MARGIN, segment, 0)

    for w in range(strips):
        for r in range(0, rows, 8):
            final[w, pl.ds(base + r, 8), :] = jnp.log(1.0 + state[MARGIN, w, pl.ds(top + r, 8), :])
    ends = [
        pltpu.make_async_copy(
            final.at[w, own, :], discharge.at[:, pl.ds(w * LANES, LANES)], out_sem.at[1, w])
        for w in range(strips)
    ]
    for store in ends:
        store.start()
    leave_all(near_copies)
    leave_all(route_copies)
    leave_all(route_mid_copies)
    for store in stores + ends:
        store.wait()


def solution(mesh):
    nrow, ncol = mesh.shape["row"], mesh.shape["col"]

    def on_device(depth, rainfall, conveyance, flow_dir, outlet):
        rows, cols = depth.shape
        strips = cols // LANES
        high = rows + 2 * MARGIN + 16
        low = rows + 32
        f32 = functools.partial(pltpu.VMEM, dtype=jnp.float32)
        dma = pltpu.SemaphoreType.DMA
        segments = PASSES // MARGIN
        return tuple(pl.pallas_call(
            functools.partial(kernel, rows, cols, nrow, ncol),
            out_shape=[jax.ShapeDtypeStruct((rows, cols), jnp.float32)] * 2,
            in_specs=[pl.BlockSpec(memory_space=pl.ANY)] * 5,
            out_specs=[pl.BlockSpec(memory_space=pl.ANY)] * 2,
            scratch_shapes=[
                f32((4, strips + 3, low, LANES)),
                pltpu.VMEM((strips, rows, LANES), jnp.int32),
                pltpu.VMEM((strips, rows, LANES), jnp.int32),
                f32((2, strips, 32, LANES)),
                f32((2, strips + 3, 32, LANES)),
                f32((strips + 1, high, LANES)),
                f32((strips + 1, high, LANES)),
                f32((strips + 3, low, LANES)),
                f32((strips + 3, low, LANES)),
                f32((8, strips + 3, high, LANES)),
                f32((MARGIN + 1, strips + 1, high, LANES)),
                f32((segments, 2, strips + 1, MARGIN, LANES)),
                f32((strips + 3, low, LANES)),
                dma((5, strips)),
                dma((2, strips)),
                dma((8,)), dma((8,)), dma((2, 2)), dma((2, 2)),
                dma((segments, 2)), dma((segments, 2)),
            ],
            compiler_params=pltpu.CompilerParams(collective_id=0, has_side_effects=True),
            name="overland",
        )(depth, rainfall, conveyance, flow_dir, outlet))

    placed = P("row", "col")
    return jax.shard_map(
        on_device, mesh=mesh, in_specs=(placed,) * 5, out_specs=(placed, placed), check_vma=False)
```

time: 39.9 us -> 33.1 us (0.83)
  Pallas kernels: 36.8 us -> 30 us
    pallas_call x1, Pallas kernels: 36.8 us -> 30 us  [on_device(): pl.pallas_call(functools.partial(kernel, rows, cols, nrow, ncol), out_sha...]
where the time goes in v2:
time: 33.1 us; the launch traced here: 32.9 us
  Pallas kernels  30 us (91%)
  local copies, waits for them, and re-layouts  2.26 us (7%)
  between operations  0.65 us (2%)
    pallas_call x1, Pallas kernels, on_device(): pl.pallas_call(functools.partial(kernel, rows, cols, nrow, ncol), out_sha...  30 us
    unnamed x4, local copies, waits for them, and re-layouts  2.26 us

profile of v2, /device:TPU:121, one launch (start us, length us, event | category | flops | bytes accessed | tf_op | source)
XLA Modules:
  0.0 32.9 jit_solution(764287617719244410)
XLA Ops:
  0.6 30.0 %overland.1 = (f32[64,512]{1,0:T(8,128)}, f32[64,512]{1,0:T(8,128)}) custom-call(f32[64,512]{1,0:T(8,128)} %depth.1, f32[64,512]{1,0:T(8,128)} %rainfall.1, f32[64,512]{1,0:T(8,128)} %conveyance.1, s32[64,512]{1,0:T(8,128)} %flow_dir.1, s32[64,512]{1,0:T(8,128)} %outlet.1), custom_call_target="tpu_custom_call" | custom-call | tf_op jit(solution)/shard_map/overland/pallas_call | solution.py:312
  30.6 0.0 copy-start
  30.6 1.6 %copy.9 = f32[64,512]{1,0:T(8,128)} copy(f32[64,512]{1,0:T(8,128)} %get-tuple-element.4) | data formatting | bytes 262144
  32.2 0.0 copy-done
  32.3 0.7 %copy.10 = f32[64,512]{1,0:T(8,128)} copy(f32[64,512]{1,0:T(8,128)S(1)} %copy-done) | data formatting | bytes 262144
Async XLA Ops:
  30.6 1.6 %copy-start = (f32[64,512]{1,0:T(8,128)S(1)}, f32[64,512]{1,0:T(8,128)}, u32[]{:S(2)}) copy-start(f32[64,512]{1,0:T(8,128)} %get-tuple-element.5) | copy-start | bytes 393220

commit v3 on v2

--- a/solution.py
+++ b/solution.py
@@ -10,7 +10,7 @@
 SUBSTEPS = 3
 PASSES = 64
 MARGIN = 32
-INNER = 16
+INNER = 24
 LANES = 128
 NEAR = 4
 MESH = pl.DeviceIdType.MESH
@@ -26,11 +26,36 @@
     return made
 
 
+def to_ring(values):
+    count = len(values)
+    lane = lax.broadcasted_iota(jnp.int32, values[0].shape, 1)
+    made = []
+    for w in range(count):
+        n = count * lane + w
+        at = n & (LANES - 1)
+        out = jnp.take_along_axis(values[0], at, axis=1)
+        for k in range(1, count):
+            out = jnp.where(n >= k * LANES, jnp.take_along_axis(values[k], at, axis=1), out)
+        made.append(out)
+    return made
+
+
+def from_ring(values, strip):
+    count = len(values)
+    n = lax.broadcasted_iota(jnp.int32, values[0].shape, 1) + strip * LANES
+    at = (n * ((1 << 18) // count + 1)) >> 18
+    which = n - count * at
+    out = jnp.take_along_axis(values[0], at, axis=1)
+    for k in range(1, count):
+        out = jnp.where(which == k, jnp.take_along_axis(values[k], at, axis=1), out)
+    return out
+
+
 def kernel(
     rows, cols, nrow, ncol,
-    depth, rainfall, conveyance, flow_dir, outlet, new_depth, discharge,
-    near, flow, out_of, pack, landed, route, level, sent, rest, masks, state, far, final,
-    in_sem, out_sem, near_ssem, near_rsem, route_ssem, route_rsem, far_ssem, far_rsem,
+    depth, rainfall, conveyance, flow_dir, outlet, new_depth, runoff,
+    near, flow, out_of, pack, landed, route, ring_route, level, sent, rest, near_masks, masks, state, far, final,
+    in_sem, near_ssem, near_rsem, route_ssem, route_rsem, far_ssem, far_rsem,
 ):
     strips = cols // LANES
     mid, left, right = strips, strips + 1, strips + 2
@@ -153,6 +178,45 @@
     start_all(near_copies)
     start_all(route_copies)
 
+    def make_masks(target, codes, w, r):
+        around = {di: codes[w, pl.ds(r - di, 8), :] for di in (-1, 0, 1)}
+        for k, (di, dj) in enumerate(OFFSETS):
+            target[k, w, pl.ds(r, 8), :] = jnp.where(
+                around[di] == jnp.float32(k + 1), jnp.float32(1.0), jnp.float32(0.0))
+
+    def inflow(r):
+        east, west, still = [], [], []
+        here = pl.ds(r, 8)
+        count = len(near_order)
+        for w in near_order:
+            x = {di: sent[w, pl.ds(r - di, 8), :] for di in (-1, 0, 1)}
+            term = [near_masks[k, w, here, :] * x[di] for k, (di, _) in enumerate(OFFSETS)]
+            east.append(term[0] + term[1] + term[7])
+            west.append(term[3] + term[4] + term[5])
+            still.append(rest[w, here, :] + term[2] + term[6])
+        east = [pltpu.roll(x, 1, 1) for x in east]
+        west = [pltpu.roll(x, LANES - 1, 1) for x in west]
+        return [
+            still[i]
+            + jnp.where(lane == 0, east[i - 1], east[i])
+            + jnp.where(lane == LANES - 1, west[(i + 1) % count], west[i])
+            for i in range(count)
+        ]
+
+    def outflow(held, w, r):
+        at = pl.ds(r, 8)
+        h = held[w, at, :]
+        factor = near[2, w, at, :] * jnp.exp(jnp.log(h) * jnp.float32(2.0 / 3.0))
+        out = h * (factor / (1.0 + factor))
+        sent[w, at, :] = out
+        rest[w, at, :] = h + near[1, w, at, :] - out
+
+    for w in range(strips):
+        for r in starts(base + 1, base + rows - 1):
+            make_masks(near_masks, near.at[3], w, r)
+        for r in range(base, base + rows, 8):
+            outflow(near.at[0], w, r)
+
     arrive_all(near_copies)
     for r in range(0, rows, 8):
         here = pl.ds(base + r, 8)
@@ -163,80 +227,65 @@
             near[a, w, pl.ds(base - 8, 8), :] = landed[0, w, pl.ds(8 + NEAR * (a - 1), 8), :]
             near[a, w, pl.ds(base + rows, 8), :] = landed[1, w, pl.ds(8 + NEAR * a, 8), :]
 
-    def make_masks(codes, shift, w, r):
-        around = {di: codes[w, pl.ds(r + shift - di, 8), :] for di in (-1, 0, 1)}
-        for k, (di, dj) in enumerate(OFFSETS):
-            masks[k, w, pl.ds(r, 8), :] = jnp.where(
-                around[di] == jnp.float32(k + 1), jnp.float32(1.0), jnp.float32(0.0))
-
-    def inflow(source, shift, order, held, r):
-        east, west, still = [], [], []
-        count = len(order)
-        for w in order:
-            x = {di: source[w, pl.ds(r + shift - di, 8), :] for di in (-1, 0, 1)}
-            term = [masks[k, w, pl.ds(r, 8), :] * x[di] for k, (di, _) in enumerate(OFFSETS)]
-            east.append(term[0] + term[1] + term[7])
-            west.append(term[3] + term[4] + term[5])
-            still.append(held[w, pl.ds(r + shift, 8), :] + term[2] + term[6])
-        east = [pltpu.roll(x, 1, 1) for x in east]
-        west = [pltpu.roll(x, LANES - 1, 1) for x in west]
-        return [
-            still[i]
-            + jnp.where(lane == 0, east[i - 1], east[i])
-            + jnp.where(lane == LANES - 1, west[(i + 1) % count], west[i])
-            for i in range(count)
-        ]
-
+    reach = starts(base - NEAR, base + rows + NEAR)
     for w in near_order:
-        for r in starts(top - NEAR, end + NEAR):
-            make_masks(near.at[3], base - top, w, r)
-    for r in starts(top + 1, end - 1):
-        make_masks(route, 0, mid, r)
+        for r in reach if w >= strips else (base - 7, base + rows - 1):
+            make_masks(near_masks, near.at[3], w, r)
     for step in range(SUBSTEPS):
-        held = near.at[0] if step == 0 else final
         for w in near_order:
-            for r in starts(base - NEAR, base + rows + NEAR):
-                at = pl.ds(r, 8)
-                h = held[w, at, :]
-                factor = near[2, w, at, :] * jnp.exp(jnp.log(h) * jnp.float32(2.0 / 3.0))
-                out = h * (factor / (1.0 + factor))
-                sent[w, at, :] = out
-                rest[w, at, :] = h + near[1, w, at, :] - out
+            for r in (base - 8, base + rows) if step == 0 and w < strips else reach:
+                outflow(near.at[0] if step == 0 else final, w, r)
         if step < SUBSTEPS - 1:
-            for r in starts(top - NEAR, end + NEAR):
-                new = inflow(sent, base - top, near_order, rest, r)
-                for w, value in zip(near_order, new):
-                    final[w, pl.ds(r + base - top, 8), :] = value
-    for r in range(top, end, 8):
-        new = inflow(sent, base - top, near_order, rest, r)
-        for w, value in enumerate(new[1:-1] + [jnp.where(lane < LANES // 2, new[-1], new[0])]):
-            level[w, pl.ds(r, 8), :] = value
-            state[0, w, pl.ds(r, 8), :] = value
+            for r in reach:
+                for w, value in zip(near_order, inflow(r)):
+                    final[w, pl.ds(r, 8), :] = value
+    for r in range(0, rows, 8):
+        new = inflow(base + r)
+        for w in range(strips):
+            new_depth[pl.ds(r, 8), pl.ds(w * LANES, LANES)] = new[1 + w]
+        ring = to_ring(new[1:-1] + [jnp.where(lane < LANES // 2, new[-1], new[0])])
+        for w, value in enumerate(ring):
+            level[w, pl.ds(top + r, 8), :] = value
+            state[0, w, pl.ds(top + r, 8), :] = value
 
     start_all(far_copies(level, 0))
-    stores = [
-        pltpu.make_async_copy(
-            level.at[w, pl.ds(top, rows), :], new_depth.at[:, pl.ds(w * LANES, LANES)], out_sem.at[0, w])
-        for w in range(strips)
-    ]
-    for store in stores:
-        store.start()
-
-    lanes = lax.broadcasted_iota(jnp.int32, (strips + 1, 8, LANES), 2)
+
+    def ring_routes(first, last):
+        for r in range(first, last, 8):
+            for w, value in enumerate(to_ring([route[w, pl.ds(r, 8), :] for w in inner_order])):
+                ring_route[w, pl.ds(r, 8), :] = value
+
+    ring_routes(top, end)
+    for w in inner_order:
+        for r in starts(top + 1, end - 1):
+            make_masks(masks, ring_route, w, r)
 
     def one_pass(p, blocks):
         for r in blocks:
+            here = pl.ds(r, 8)
             x = {di: state[p, :, pl.ds(r - di, 8), :] for di in (-1, 0, 1)}
-            term = [masks[k, pl.ds(0, strips + 1), pl.ds(r, 8), :] * x[di] for k, (di, _) in enumerate(OFFSETS)]
-            east = pltpu.roll(term[0] + term[1] + term[7], 1, 2)
-            west = pltpu.roll(term[3] + term[4] + term[5], LANES - 1, 2)
-            still = level[:, pl.ds(r, 8), :] + term[2] + term[6]
-            before = jnp.concatenate([east[strips:], east[:strips]], axis=0)
-            after = jnp.concatenate([west[1:], west[:1]], axis=0)
-            value = still + jnp.where(lanes == 0, before, east) + jnp.where(lanes == LANES - 1, after, west)
-            state[p + 1, :, pl.ds(r, 8), :] = value
+            term = [masks[k, :, here, :] * x[di] for k, (di, _) in enumerate(OFFSETS)]
+            east = term[0] + term[1] + term[7]
+            west = term[3] + term[4] + term[5]
+            still = level[:, here, :] + term[2] + term[6]
+            east = jnp.concatenate([pltpu.roll(east[strips:], 1, 2), east[:strips]], axis=0)
+            west = jnp.concatenate([west[1:], pltpu.roll(west[:1], LANES - 1, 2)], axis=0)
+            value = still + east + west
+            state[p + 1, :, here, :] = value
             if p == MARGIN - 1:
-                state[0, :, pl.ds(r, 8), :] = value
+                state[0, :, here, :] = value
+
+    def halo(seg, half):
+        first = end if half else top - MARGIN
+        for w in inner_order:
+            for r in range(0, MARGIN, 8):
+                state[0, w, pl.ds(first + r, 8), :] = far[seg, half, w, pl.ds(r, 8), :]
+
+        @pl.when(seg == 0)
+        def _():
+            for w in inner_order:
+                for r in range(0, MARGIN, 8):
+                    level[w, pl.ds(first + r, 8), :] = far[0, half, w, pl.ds(r, 8), :]
 
     def segment(seg, carry):
         for p in range(INNER):
@@ -246,26 +295,16 @@
         def _():
             arrive_all(route_copies)
             arrive_all(route_mid_copies)
+            ring_routes(top - MARGIN, top)
+            ring_routes(end, end + MARGIN)
             for w in inner_order:
-                for r in range(top - MARGIN, top + (8 if w == mid else 0), 8):
-                    make_masks(route, 0, w, r)
-                for r in range(end - (8 if w == mid else 0), end + MARGIN, 8):
-                    make_masks(route, 0, w, r)
+                for r in (*range(top - MARGIN, top + 8, 8), *range(end - 8, end + MARGIN, 8)):
+                    make_masks(masks, ring_route, w, r)
 
         arrive_all(far_copies(level, seg))
         leave_all(far_copies(level, seg))
-        for w in inner_order:
-            for r in range(0, MARGIN, 8):
-                state[0, w, pl.ds(top - MARGIN + r, 8), :] = far[seg, 0, w, pl.ds(r, 8), :]
-                state[0, w, pl.ds(end + r, 8), :] = far[seg, 1, w, pl.ds(r, 8), :]
-
-        @pl.when(seg == 0)
-        def _():
-            for w in inner_order:
-                for r in range(0, MARGIN, 8):
-                    level[w, pl.ds(top - MARGIN + r, 8), :] = far[0, 0, w, pl.ds(r, 8), :]
-                    level[w, pl.ds(end + r, 8), :] = far[0, 1, w, pl.ds(r, 8), :]
-
+        halo(seg, 0)
+        halo(seg, 1)
         for p in range(MARGIN):
             above, below = top - MARGIN + p + 1, end + MARGIN - p - 1
             if p < INNER:
@@ -281,21 +320,26 @@
 
     lax.fori_loop(0, PASSES // MARGIN, segment, 0)
 
-    for w in range(strips):
+    for w in inner_order:
         for r in range(0, rows, 8):
-            final[w, pl.ds(base + r, 8), :] = jnp.log(1.0 + state[MARGIN, w, pl.ds(top + r, 8), :])
-    ends = [
-        pltpu.make_async_copy(
-            final.at[w, own, :], discharge.at[:, pl.ds(w * LANES, LANES)], out_sem.at[1, w])
-        for w in range(strips)
-    ]
-    for store in ends:
-        store.start()
+            runoff[w, pl.ds(r, 8), :] = state[MARGIN, w, pl.ds(top + r, 8), :]
     leave_all(near_copies)
     leave_all(route_copies)
     leave_all(route_mid_copies)
-    for store in stores + ends:
-        store.wait()
+
+
+def finish(level, runoff, new_depth, discharge, logs, sems):
+    first = pltpu.make_async_copy(level, new_depth, sems.at[0])
+    first.start()
+    rows, cols = level.shape
+    for r in range(0, rows, 8):
+        ring = [jnp.log(1.0 + runoff[w, pl.ds(r, 8), :]) for w in range(runoff.shape[0])]
+        for w in range(cols // LANES):
+            logs[pl.ds(r, 8), pl.ds(w * LANES, LANES)] = from_ring(ring, w)
+    second = pltpu.make_async_copy(logs, discharge, sems.at[1])
+    second.start()
+    first.wait()
+    second.wait()
 
 
 def solution(mesh):
@@ -309,11 +353,16 @@
         f32 = functools.partial(pltpu.VMEM, dtype=jnp.float32)
         dma = pltpu.SemaphoreType.DMA
         segments = PASSES // MARGIN
-        return tuple(pl.pallas_call(
+        pin = lambda x: pltpu.with_memory_space_constraint(x, pltpu.HBM)
+        depth, rainfall, conveyance, flow_dir, outlet = map(pin, (depth, rainfall, conveyance, flow_dir, outlet))
+        level, runoff = pl.pallas_call(
             functools.partial(kernel, rows, cols, nrow, ncol),
-            out_shape=[jax.ShapeDtypeStruct((rows, cols), jnp.float32)] * 2,
+            out_shape=[
+                jax.ShapeDtypeStruct((rows, cols), jnp.float32),
+                jax.ShapeDtypeStruct((strips + 1, rows, LANES), jnp.float32),
+            ],
             in_specs=[pl.BlockSpec(memory_space=pl.ANY)] * 5,
-            out_specs=[pl.BlockSpec(memory_space=pl.ANY)] * 2,
+            out_specs=[pl.BlockSpec(memory_space=pltpu.VMEM)] * 2,
             scratch_shapes=[
                 f32((4, strips + 3, low, LANES)),
                 pltpu.VMEM((strips, rows, LANES), jnp.int32),
@@ -322,20 +371,31 @@
                 f32((2, strips + 3, 32, LANES)),
                 f32((strips + 1, high, LANES)),
                 f32((strips + 1, high, LANES)),
+                f32((strips + 1, high, LANES)),
                 f32((strips + 3, low, LANES)),
                 f32((strips + 3, low, LANES)),
-                f32((8, strips + 3, high, LANES)),
+                f32((8, strips + 3, low, LANES)),
+                f32((8, strips + 1, high, LANES)),
                 f32((MARGIN + 1, strips + 1, high, LANES)),
                 f32((segments, 2, strips + 1, MARGIN, LANES)),
                 f32((strips + 3, low, LANES)),
                 dma((5, strips)),
-                dma((2, strips)),
                 dma((8,)), dma((8,)), dma((2, 2)), dma((2, 2)),
                 dma((segments, 2)), dma((segments, 2)),
             ],
-            compiler_params=pltpu.CompilerParams(collective_id=0, has_side_effects=True),
+            compiler_params=pltpu.CompilerParams(
+                collective_id=0, has_side_effects=True, vmem_limit_bytes=32 * 2**20),
             name="overland",
-        )(depth, rainfall, conveyance, flow_dir, outlet))
+        )(depth, rainfall, conveyance, flow_dir, outlet)
+        return tuple(pl.pallas_call(
+            finish,
+            out_shape=[jax.ShapeDtypeStruct((rows, cols), jnp.float32)] * 2,
+            in_specs=[pl.BlockSpec(memory_space=pltpu.VMEM)] * 2,
+            out_specs=[pl.BlockSpec(memory_space=pl.ANY)] * 2,
+            scratch_shapes=[f32((rows, cols)), dma((2,))],
+            compiler_params=pltpu.CompilerParams(vmem_limit_bytes=4 * 2**20),
+            name="finish",
+        )(level, runoff))
 
     placed = P("row", "col")
     return jax.shard_map(

time: 33.1 us -> 29.6 us (0.89)
  local copies, waits for them, and re-layouts: 2.26 us -> 0 us
  Pallas kernels: 30 us -> 28.7 us
    pallas_call x1, Pallas kernels: 30 us -> 27.7 us  [on_device(): pl.pallas_call(functools.partial(kernel, rows, cols, nrow, ncol), out_sha...]
    unnamed x4 -> x0, local copies, waits for them, and re-layouts: 2.26 us -> none
    pallas_call x0 -> x1, Pallas kernels: none -> 1.03 us  [on_device(): pl.pallas_call(finish, out_shape=[jax.ShapeDtypeStruct((rows, cols), jnp....]
where the time goes in v3:
time: 29.6 us; the launch traced here: 29.4 us
  Pallas kernels  28.7 us (97%)
  between operations  0.64 us (2%)
    pallas_call x1, Pallas kernels, on_device(): pl.pallas_call(functools.partial(kernel, rows, cols, nrow, ncol), out_sha...  27.7 us
    pallas_call x1, Pallas kernels, on_device(): pl.pallas_call(finish, out_shape=[jax.ShapeDtypeStruct((rows, cols), jnp....  1.03 us

profile of v3, /device:TPU:121, one launch (start us, length us, event | category | flops | bytes accessed | tf_op | source)
XLA Modules:
  0.0 29.4 jit_solution(16425398553884182204)
XLA Ops:
  0.6 27.7 %overland.1 = (f32[64,512]{1,0:T(8,128)S(1)}, f32[5,64,128]{2,1,0:T(8,128)S(1)}) custom-call(f32[64,512]{1,0:T(8,128)} %depth.1, f32[64,512]{1,0:T(8,128)} %rainfall.1, f32[64,512]{1,0:T(8,128)} %conveyance.1, s32[64,512]{1,0:T(8,128)} %flow_dir.1, s32[64,512]{1,0:T(8,128)} %outlet.1), custom_call_target="tpu_custom_call" | custom-call | tf_op jit(solution)/shard_map/overland/pallas_call | solution.py:358
  28.3 1.0 %finish.1 = (f32[64,512]{1,0:T(8,128)}, f32[64,512]{1,0:T(8,128)}) custom-call(f32[64,512]{1,0:T(8,128)S(1)} %get-tuple-element.4.level, f32[5,64,128]{2,1,0:T(8,128)S(1)} %get-tuple-element.5.runoff), custom_call_target="tpu_custom_call" | custom-call | tf_op jit(solution)/shard_map/finish/pallas_call | solution.py:390

commit v4 on v3

--- a/solution.py
+++ b/solution.py
@@ -10,7 +10,6 @@
 SUBSTEPS = 3
 PASSES = 64
 MARGIN = 32
-INNER = 24
 LANES = 128
 NEAR = 4
 MESH = pl.DeviceIdType.MESH
@@ -243,11 +242,18 @@
         new = inflow(base + r)
         for w in range(strips):
             new_depth[pl.ds(r, 8), pl.ds(w * LANES, LANES)] = new[1 + w]
-        ring = to_ring(new[1:-1] + [jnp.where(lane < LANES // 2, new[-1], new[0])])
-        for w, value in enumerate(ring):
-            level[w, pl.ds(top + r, 8), :] = value
-            state[0, w, pl.ds(top + r, 8), :] = value
-
+            final[w, pl.ds(base + r, 8), :] = new[1 + w]
+        final[mid, pl.ds(base + r, 8), :] = jnp.where(lane < LANES // 2, new[-1], new[0])
+
+    def level_ring(step, carry):
+        for half in range(0, rows // 2, 8):
+            r = pl.multiple_of(step * (rows // 2), 8) + half
+            for w, value in enumerate(to_ring([final[w, pl.ds(base + r, 8), :] for w in inner_order])):
+                level[w, pl.ds(top + r, 8), :] = value
+                state[0, w, pl.ds(top + r, 8), :] = value
+        return carry
+
+    lax.fori_loop(0, 2, level_ring, 0)
     start_all(far_copies(level, 0))
 
     def ring_routes(first, last):
@@ -287,9 +293,22 @@
                 for r in range(0, MARGIN, 8):
                     level[w, pl.ds(first + r, 8), :] = far[0, half, w, pl.ds(r, 8), :]
 
+    def top_band(seg):
+        arrive_all(far_copies(level, seg)[1:])
+        halo(seg, 0)
+        for p in range(MARGIN):
+            one_pass(p, starts(top - MARGIN + p + 1, top + p + 1)[::-1])
+
+    def bottom_band(seg):
+        arrive_all(far_copies(level, seg)[:1])
+        halo(seg, 1)
+        for p in range(MARGIN):
+            one_pass(p, starts(end - p - 1, end + MARGIN - p - 1))
+
     def segment(seg, carry):
-        for p in range(INNER):
-            one_pass(p, starts(top + p + 1, end - p - 1))
+        for p in range(rows // 2 - 1):
+            here, stop = top + p + 1, end - p - 1
+            one_pass(p, starts(here, stop) if stop - here >= 8 else [here + (stop - here) // 2 - 4])
 
         @pl.when(seg == 0)
         def _():
@@ -300,21 +319,19 @@
             for w in inner_order:
                 for r in (*range(top - MARGIN, top + 8, 8), *range(end - 8, end + MARGIN, 8)):
                     make_masks(masks, ring_route, w, r)
-
-        arrive_all(far_copies(level, seg))
+            top_band(0)
+            start_all(far_copies(state.at[MARGIN], 1)[:1])
+
         leave_all(far_copies(level, seg))
-        halo(seg, 0)
-        halo(seg, 1)
-        for p in range(MARGIN):
-            above, below = top - MARGIN + p + 1, end + MARGIN - p - 1
-            if p < INNER:
-                one_pass(p, starts(above, above + MARGIN) + starts(below - MARGIN, below))
-            else:
-                one_pass(p, starts(above, below))
+        bottom_band(seg)
 
         @pl.when(seg == 0)
         def _():
-            start_all(far_copies(state.at[MARGIN], 1))
+            start_all(far_copies(state.at[MARGIN], 1)[1:])
+
+        @pl.when(seg == 1)
+        def _():
+            top_band(1)
 
         return carry
 

time: 29.6 us -> 31.6 us (1.068)
  Pallas kernels: 28.7 us -> 30.8 us
    pallas_call x1, Pallas kernels: 27.7 us -> 29.8 us  [on_device(): pl.pallas_call(functools.partial(kernel, rows, cols, nrow, ncol), out_sha...]
where the time goes in v4:
time: 31.6 us; the launch traced here: 31.4 us
  Pallas kernels  30.8 us (97%)
  between operations  0.64 us (2%)
    pallas_call x1, Pallas kernels, on_device(): pl.pallas_call(functools.partial(kernel, rows, cols, nrow, ncol), out_sha...  29.8 us
    pallas_call x1, Pallas kernels, on_device(): pl.pallas_call(finish, out_shape=[jax.ShapeDtypeStruct((rows, cols), jnp....  1.03 us

profile of v4, /device:TPU:121, one launch (start us, length us, event | category | flops | bytes accessed | tf_op | source)
XLA Modules:
  0.0 31.4 jit_solution(16359181573888975252)
XLA Ops:
  0.6 29.8 %overland.1 = (f32[64,512]{1,0:T(8,128)S(1)}, f32[5,64,128]{2,1,0:T(8,128)S(1)}) custom-call(f32[64,512]{1,0:T(8,128)} %depth.1, f32[64,512]{1,0:T(8,128)} %rainfall.1, f32[64,512]{1,0:T(8,128)} %conveyance.1, s32[64,512]{1,0:T(8,128)} %flow_dir.1, s32[64,512]{1,0:T(8,128)} %outlet.1), custom_call_target="tpu_custom_call" | custom-call | tf_op jit(solution)/shard_map/overland/pallas_call | solution.py:375
  30.4 1.0 %finish.1 = (f32[64,512]{1,0:T(8,128)}, f32[64,512]{1,0:T(8,128)}) custom-call(f32[64,512]{1,0:T(8,128)S(1)} %get-tuple-element.4.level, f32[5,64,128]{2,1,0:T(8,128)S(1)} %get-tuple-element.5.runoff), custom_call_target="tpu_custom_call" | custom-call | tf_op jit(solution)/shard_map/finish/pallas_call | solution.py:407

commit v5 on v4

--- a/solution.py
+++ b/solution.py
@@ -1,4 +1,5 @@
 import functools
+import math
 
 import jax
 import jax.numpy as jnp
@@ -53,7 +54,7 @@
 def kernel(
     rows, cols, nrow, ncol,
     depth, rainfall, conveyance, flow_dir, outlet, new_depth, runoff,
-    near, flow, out_of, pack, landed, route, ring_route, level, sent, rest, near_masks, masks, state, far, final,
+    near, plain, flow, out_of, pack, landed, route, ring_route, level, sent, rest, near_masks, masks, state, far, final,
     in_sem, near_ssem, near_rsem, route_ssem, route_rsem, far_ssem, far_rsem,
 ):
     strips = cols // LANES
@@ -72,34 +73,6 @@
         r, c = me_r + dr, me_c + dc
         return (r >= 0) & (r < nrow) & (c >= 0) & (c < ncol)
 
-    loads = []
-    for a, (source, target) in enumerate((
-        (flow_dir, flow), (outlet, out_of), (depth, near.at[0]), (rainfall, near.at[1]), (conveyance, near.at[2]),
-    )):
-        for w in range(strips):
-            loads.append(pltpu.make_async_copy(
-                source.at[:, pl.ds(w * LANES, LANES)],
-                target.at[w, pl.ds(0, rows) if a < 2 else own, :], in_sem.at[a, w]))
-    for load in loads:
-        load.start()
-
-    def clear(ref, first, last):
-        for r in range(first, last, 8):
-            ref[pl.ds(r, 8), :] = zero
-
-    for half in range(2):
-        for w in near_order:
-            clear(landed.at[half, w], 8, 8 + 4 * NEAR)
-        for seg in range(PASSES // MARGIN):
-            for w in inner_order:
-                clear(far.at[seg, half, w], 0, MARGIN)
-    for a in range(4):
-        for w in (left, right):
-            clear(near.at[a, w], base, base + rows)
-    for w in inner_order:
-        clear(route.at[w], top - MARGIN, top)
-        clear(route.at[w], end, end + MARGIN)
-
     barrier = pltpu.get_barrier_semaphore()
     neighbours = jnp.int32(0)
     for dr, dc in SIDES:
@@ -109,6 +82,42 @@
         @pl.when(here)
         def _():
             pl.semaphore_signal(barrier, inc=1, device_id=(me_r + dr, me_c + dc), device_id_type=MESH)
+
+    loads = [
+        pltpu.make_async_copy(source, target, in_sem.at[a])
+        for a, (source, target) in enumerate((
+            (flow_dir, flow), (outlet, out_of), (conveyance, plain.at[2]), (depth, plain.at[0]), (rainfall, plain.at[1]),
+        ))
+    ]
+    for load in loads:
+        load.start()
+
+    def clear(ref, first, last):
+        for r in range(first, last, 8):
+            ref[pl.ds(r, 8), :] = zero
+
+    for half, dr in enumerate((-1, 1)):
+        @pl.when(jnp.logical_not(present(dr, 0)))
+        def _():
+            for seg in range(PASSES // MARGIN):
+                for w in inner_order:
+                    clear(far.at[seg, half, w], 0, MARGIN)
+            for w in range(strips):
+                clear(landed.at[half, w], 8, 8 + 4 * NEAR)
+            for w in inner_order:
+                first = end if half else top - MARGIN
+                clear(route.at[w], first, first + MARGIN)
+
+        for w, dc in ((left, -1), (right, 1)):
+            @pl.when(jnp.logical_not(present(dr, dc)))
+            def _():
+                clear(landed.at[half, w], 8, 8 + 4 * NEAR)
+
+    for w, dc in ((left, -1), (right, 1)):
+        @pl.when(jnp.logical_not(present(0, dc)))
+        def _():
+            for a in range(4):
+                clear(near.at[a, w], base, base + rows)
 
     def remote(side, src, dst, ssem, rsem):
         return side, pltpu.make_async_remote_copy(
@@ -161,13 +170,15 @@
         load.wait()
     for w in range(strips):
         for r in range(0, rows, 8):
-            at, here = pl.ds(r, 8), pl.ds(base + r, 8)
-            code = flow[w, at, :]
-            kind = jnp.where(out_of[w, at, :] == 1, 0, code + 1).astype(jnp.float32)
+            at, here = (pl.ds(r, 8), pl.ds(w * LANES, LANES)), pl.ds(base + r, 8)
+            code = flow[at]
+            kind = jnp.where(out_of[at] == 1, 0, code + 1).astype(jnp.float32)
             near[3, w, here, :] = kind
             route[w, pl.ds(top + r, 8), :] = kind
             length = jnp.where(code % 2 == 1, jnp.float32(0.70710678), jnp.float32(1.0))
-            near[2, w, here, :] = near[2, w, here, :] * length
+            near[2, w, here, :] = plain[2, at[0], at[1]] * length
+            for a in range(2):
+                near[a, w, here, :] = plain[a, at[0], at[1]]
         for a in range(4):
             pack[0, w, pl.ds(8 + NEAR * a, 8), :] = near[a, w, pl.ds(base, 8), :]
         for a in reversed(range(4)):
@@ -205,7 +216,7 @@
     def outflow(held, w, r):
         at = pl.ds(r, 8)
         h = held[w, at, :]
-        factor = near[2, w, at, :] * jnp.exp(jnp.log(h) * jnp.float32(2.0 / 3.0))
+        factor = near[2, w, at, :] * jnp.exp2(jnp.log(h) * jnp.float32(2.0 / 3.0 / math.log(2.0)))
         out = h * (factor / (1.0 + factor))
         sent[w, at, :] = out
         rest[w, at, :] = h + near[1, w, at, :] - out
@@ -293,17 +304,9 @@
                 for r in range(0, MARGIN, 8):
                     level[w, pl.ds(first + r, 8), :] = far[0, half, w, pl.ds(r, 8), :]
 
-    def top_band(seg):
-        arrive_all(far_copies(level, seg)[1:])
-        halo(seg, 0)
+    def bands():
         for p in range(MARGIN):
-            one_pass(p, starts(top - MARGIN + p + 1, top + p + 1)[::-1])
-
-    def bottom_band(seg):
-        arrive_all(far_copies(level, seg)[:1])
-        halo(seg, 1)
-        for p in range(MARGIN):
-            one_pass(p, starts(end - p - 1, end + MARGIN - p - 1))
+            one_pass(p, starts(top - MARGIN + p + 1, top + p + 1) + starts(end - p - 1, end + MARGIN - p - 1))
 
     def segment(seg, carry):
         for p in range(rows // 2 - 1):
@@ -319,19 +322,16 @@
             for w in inner_order:
                 for r in (*range(top - MARGIN, top + 8, 8), *range(end - 8, end + MARGIN, 8)):
                     make_masks(masks, ring_route, w, r)
-            top_band(0)
-            start_all(far_copies(state.at[MARGIN], 1)[:1])
-
+
+        arrive_all(far_copies(level, seg))
         leave_all(far_copies(level, seg))
-        bottom_band(seg)
+        halo(seg, 0)
+        halo(seg, 1)
+        bands()
 
         @pl.when(seg == 0)
         def _():
-            start_all(far_copies(state.at[MARGIN], 1)[1:])
-
-        @pl.when(seg == 1)
-        def _():
-            top_band(1)
+            start_all(far_copies(state.at[MARGIN], 1))
 
         return carry
 
@@ -349,14 +349,17 @@
     first = pltpu.make_async_copy(level, new_depth, sems.at[0])
     first.start()
     rows, cols = level.shape
-    for r in range(0, rows, 8):
-        ring = [jnp.log(1.0 + runoff[w, pl.ds(r, 8), :]) for w in range(runoff.shape[0])]
-        for w in range(cols // LANES):
-            logs[pl.ds(r, 8), pl.ds(w * LANES, LANES)] = from_ring(ring, w)
-    second = pltpu.make_async_copy(logs, discharge, sems.at[1])
-    second.start()
-    first.wait()
-    second.wait()
+    made = [first]
+    for part in range(4):
+        for r in range(part * rows // 4, (part + 1) * rows // 4, 8):
+            ring = [jnp.log(1.0 + runoff[w, pl.ds(r, 8), :]) for w in range(runoff.shape[0])]
+            for w in range(cols // LANES):
+                logs[pl.ds(r, 8), pl.ds(w * LANES, LANES)] = from_ring(ring, w)
+        at = pl.ds(part * rows // 4, rows // 4)
+        made.append(pltpu.make_async_copy(logs.at[at, :], discharge.at[at, :], sems.at[1 + part]))
+        made[-1].start()
+    for copy in made:
+        copy.wait()
 
 
 def solution(mesh):
@@ -382,8 +385,9 @@
             out_specs=[pl.BlockSpec(memory_space=pltpu.VMEM)] * 2,
             scratch_shapes=[
                 f32((4, strips + 3, low, LANES)),
-                pltpu.VMEM((strips, rows, LANES), jnp.int32),
-                pltpu.VMEM((strips, rows, LANES), jnp.int32),
+                f32((3, rows, cols)),
+                pltpu.VMEM((rows, cols), jnp.int32),
+                pltpu.VMEM((rows, cols), jnp.int32),
                 f32((2, strips, 32, LANES)),
                 f32((2, strips + 3, 32, LANES)),
                 f32((strips + 1, high, LANES)),
@@ -396,7 +400,7 @@
                 f32((MARGIN + 1, strips + 1, high, LANES)),
                 f32((segments, 2, strips + 1, MARGIN, LANES)),
                 f32((strips + 3, low, LANES)),
-                dma((5, strips)),
+                dma((5,)),
                 dma((8,)), dma((8,)), dma((2, 2)), dma((2, 2)),
                 dma((segments, 2)), dma((segments, 2)),
             ],
@@ -409,7 +413,7 @@
             out_shape=[jax.ShapeDtypeStruct((rows, cols), jnp.float32)] * 2,
             in_specs=[pl.BlockSpec(memory_space=pltpu.VMEM)] * 2,
             out_specs=[pl.BlockSpec(memory_space=pl.ANY)] * 2,
-            scratch_shapes=[f32((rows, cols)), dma((2,))],
+            scratch_shapes=[f32((rows, cols)), dma((5,))],
             compiler_params=pltpu.CompilerParams(vmem_limit_bytes=4 * 2**20),
             name="finish",
         )(level, runoff))

time: 31.6 us -> 28.6 us (0.905)
  Pallas kernels: 30.8 us -> 27.8 us
    pallas_call x1, Pallas kernels: 29.8 us -> 26.8 us  [on_device(): pl.pallas_call(functools.partial(kernel, rows, cols, nrow, ncol), out_sha...]
where the time goes in v5:
time: 28.6 us; the launch traced here: 28.5 us
  Pallas kernels  27.8 us (97%)
  between operations  0.64 us (2%)
    pallas_call x1, Pallas kernels, on_device(): pl.pallas_call(functools.partial(kernel, rows, cols, nrow, ncol), out_sha...  26.8 us
    pallas_call x1, Pallas kernels, on_device(): pl.pallas_call(finish, out_shape=[jax.ShapeDtypeStruct((rows, cols), jnp....  1.02 us

profile of v5, /device:TPU:121, one launch (start us, length us, event | category | flops | bytes accessed | tf_op | source)
XLA Modules:
  0.0 28.5 jit_solution(5662108141360257530)
XLA Ops:
  0.6 26.8 %overland.1 = (f32[64,512]{1,0:T(8,128)S(1)}, f32[5,64,128]{2,1,0:T(8,128)S(1)}) custom-call(f32[64,512]{1,0:T(8,128)} %depth.1, f32[64,512]{1,0:T(8,128)} %rainfall.1, f32[64,512]{1,0:T(8,128)} %conveyance.1, s32[64,512]{1,0:T(8,128)} %flow_dir.1, s32[64,512]{1,0:T(8,128)} %outlet.1), custom_call_target="tpu_custom_call" | custom-call | tf_op jit(solution)/shard_map/overland/pallas_call | solution.py:378
  27.5 1.0 %finish.1 = (f32[64,512]{1,0:T(8,128)}, f32[64,512]{1,0:T(8,128)}) custom-call(f32[64,512]{1,0:T(8,128)S(1)} %get-tuple-element.4.level, f32[5,64,128]{2,1,0:T(8,128)S(1)} %get-tuple-element.5.runoff), custom_call_target="tpu_custom_call" | custom-call | tf_op jit(solution)/shard_map/finish/pallas_call | solution.py:411

commit v6 on v5

--- a/solution.py
+++ b/solution.py
@@ -256,15 +256,13 @@
             final[w, pl.ds(base + r, 8), :] = new[1 + w]
         final[mid, pl.ds(base + r, 8), :] = jnp.where(lane < LANES // 2, new[-1], new[0])
 
-    def level_ring(step, carry):
-        for half in range(0, rows // 2, 8):
-            r = pl.multiple_of(step * (rows // 2), 8) + half
+    @pl.when(me_r >= 0)
+    def _():
+        for r in range(0, rows, 8):
             for w, value in enumerate(to_ring([final[w, pl.ds(base + r, 8), :] for w in inner_order])):
                 level[w, pl.ds(top + r, 8), :] = value
                 state[0, w, pl.ds(top + r, 8), :] = value
-        return carry
-
-    lax.fori_loop(0, 2, level_ring, 0)
+
     start_all(far_copies(level, 0))
 
     def ring_routes(first, last):
@@ -277,41 +275,89 @@
         for r in starts(top + 1, end - 1):
             make_masks(masks, ring_route, w, r)
 
+    sub = lax.broadcasted_iota(jnp.int32, (strips + 1, 8, LANES), 1)
+
+    def down(x, before, n):
+        return jnp.where(sub < n, pltpu.roll(before, n, 1), pltpu.roll(x, n, 1))
+
+    def up(x, after, n):
+        return jnp.where(sub < 8 - n, pltpu.roll(x, 8 - n, 1), pltpu.roll(after, 8 - n, 1))
+
+    def flow_into(x, r):
+        here = pl.ds(r, 8)
+        term = [masks[k, :, here, :] * x[di] for k, (di, _) in enumerate(OFFSETS)]
+        east = term[0] + term[1] + term[7]
+        west = term[3] + term[4] + term[5]
+        still = level[:, here, :] + term[2] + term[6]
+        east = jnp.concatenate([pltpu.roll(east[strips:], 1, 2), east[:strips]], axis=0)
+        west = jnp.concatenate([west[1:], pltpu.roll(west[:1], LANES - 1, 2)], axis=0)
+        return still + east + west
+
     def one_pass(p, blocks):
+        made = []
         for r in blocks:
-            here = pl.ds(r, 8)
-            x = {di: state[p, :, pl.ds(r - di, 8), :] for di in (-1, 0, 1)}
-            term = [masks[k, :, here, :] * x[di] for k, (di, _) in enumerate(OFFSETS)]
-            east = term[0] + term[1] + term[7]
-            west = term[3] + term[4] + term[5]
-            still = level[:, here, :] + term[2] + term[6]
-            east = jnp.concatenate([pltpu.roll(east[strips:], 1, 2), east[:strips]], axis=0)
-            west = jnp.concatenate([west[1:], pltpu.roll(west[:1], LANES - 1, 2)], axis=0)
-            value = still + east + west
-            state[p + 1, :, here, :] = value
-            if p == MARGIN - 1:
-                state[0, :, here, :] = value
-
-    def halo(seg, half):
-        first = end if half else top - MARGIN
-        for w in inner_order:
+            made.append(flow_into({di: state[p, :, pl.ds(r - di, 8), :] for di in (-1, 0, 1)}, r))
+            state[p + 1, :, pl.ds(r, 8), :] = made[-1]
+        return made
+
+    def interior():
+        for p in range(rows // 4 - 1):
+            one_pass(p, starts(top + p + 1, end - p - 1))
+        for first in range(rows // 4 - 1, rows // 2 - 1, 4):
+            blocks = list(range(top + first + 1, end - first - 1, 8))
+            held = one_pass(first, blocks)
+            for p in range(first + 1, first + 4):
+                new = []
+                for b, r in enumerate(blocks):
+                    new.append(flow_into({
+                        1: down(held[b], held[max(b - 1, 0)], 1),
+                        0: held[b],
+                        -1: up(held[b], held[min(b + 1, len(held) - 1)], 1),
+                    }, r))
+                    state[p + 1, :, pl.ds(r, 8), :] = new[-1]
+                held = new
+
+    def finish_band(held, first):
+        for b, value in enumerate(held):
+            for s in (0, MARGIN):
+                state[s, :, pl.ds(first + 8 * b, 8), :] = value
+
+    def top_band(seg):
+        arrive_all(far_copies(level, seg)[1:])
+        copy_level(seg, 0, top - MARGIN)
+        held = [far[seg, 0, :, pl.ds(r, 8), :] for r in range(0, MARGIN, 8)]
+        for p in range(MARGIN):
+            held.append(state[p, :, pl.ds(top + p, 8), :])
+            new = []
+            for b in range(MARGIN // 8):
+                new.append(flow_into({
+                    1: held[b], 0: up(held[b], held[b + 1], 1), -1: up(held[b], held[b + 1], 2),
+                }, top - MARGIN + p + 1 + 8 * b))
+            held = new
+        finish_band(held, top)
+
+    def bottom_band(seg):
+        arrive_all(far_copies(level, seg)[:1])
+        copy_level(seg, 1, end)
+        held = [far[seg, 1, :, pl.ds(r, 8), :] for r in range(0, MARGIN, 8)]
+        for p in range(MARGIN):
+            held.insert(0, state[p, :, pl.ds(end - p - 8, 8), :])
+            new = []
+            for b in range(MARGIN // 8):
+                new.append(flow_into({
+                    1: down(held[b + 1], held[b], 2), 0: down(held[b + 1], held[b], 1), -1: held[b + 1],
+                }, end - p - 1 + 8 * b))
+            held = new
+        finish_band(held, end - MARGIN)
+
+    def copy_level(seg, half, first):
+        @pl.when(seg == 0)
+        def _():
             for r in range(0, MARGIN, 8):
-                state[0, w, pl.ds(first + r, 8), :] = far[seg, half, w, pl.ds(r, 8), :]
-
-        @pl.when(seg == 0)
-        def _():
-            for w in inner_order:
-                for r in range(0, MARGIN, 8):
-                    level[w, pl.ds(first + r, 8), :] = far[0, half, w, pl.ds(r, 8), :]
-
-    def bands():
-        for p in range(MARGIN):
-            one_pass(p, starts(top - MARGIN + p + 1, top + p + 1) + starts(end - p - 1, end + MARGIN - p - 1))
+                level[:, pl.ds(first + r, 8), :] = far[0, half, :, pl.ds(r, 8), :]
 
     def segment(seg, carry):
-        for p in range(rows // 2 - 1):
-            here, stop = top + p + 1, end - p - 1
-            one_pass(p, starts(here, stop) if stop - here >= 8 else [here + (stop - here) // 2 - 4])
+        interior()
 
         @pl.when(seg == 0)
         def _():
@@ -322,16 +368,19 @@
             for w in inner_order:
                 for r in (*range(top - MARGIN, top + 8, 8), *range(end - 8, end + MARGIN, 8)):
                     make_masks(masks, ring_route, w, r)
-
-        arrive_all(far_copies(level, seg))
+            top_band(0)
+            start_all(far_copies(state.at[MARGIN], 1)[:1])
+
         leave_all(far_copies(level, seg))
-        halo(seg, 0)
-        halo(seg, 1)
-        bands()
+        bottom_band(seg)
 
         @pl.when(seg == 0)
         def _():
-            start_all(far_copies(state.at[MARGIN], 1))
+            start_all(far_copies(state.at[MARGIN], 1)[1:])
+
+        @pl.when(seg == 1)
+        def _():
+            top_band(1)
 
         return carry
 

time: 28.6 us -> 30.6 us (1.070)
  Pallas kernels: 27.8 us -> 29.8 us
    pallas_call x1, Pallas kernels: 26.8 us -> 28.8 us  [on_device(): pl.pallas_call(functools.partial(kernel, rows, cols, nrow, ncol), out_sha...]
where the time goes in v6:
time: 30.6 us; the launch traced here: 30.5 us
  Pallas kernels  29.8 us (97%)
  between operations  0.64 us (2%)
    pallas_call x1, Pallas kernels, on_device(): pl.pallas_call(functools.partial(kernel, rows, cols, nrow, ncol), out_sha...  28.8 us
    pallas_call x1, Pallas kernels, on_device(): pl.pallas_call(finish, out_shape=[jax.ShapeDtypeStruct((rows, cols), jnp....  1.02 us

profile of v6, /device:TPU:121, one launch (start us, length us, event | category | flops | bytes accessed | tf_op | source)
XLA Modules:
  0.0 30.5 jit_solution(12756183417126487850)
XLA Ops:
  0.6 28.8 %overland.1 = (f32[64,512]{1,0:T(8,128)S(1)}, f32[5,64,128]{2,1,0:T(8,128)S(1)}) custom-call(f32[64,512]{1,0:T(8,128)} %depth.1, f32[64,512]{1,0:T(8,128)} %rainfall.1, f32[64,512]{1,0:T(8,128)} %conveyance.1, s32[64,512]{1,0:T(8,128)} %flow_dir.1, s32[64,512]{1,0:T(8,128)} %outlet.1), custom_call_target="tpu_custom_call" | custom-call | tf_op jit(solution)/shard_map/overland/pallas_call | solution.py:427
  29.5 1.0 %finish.1 = (f32[64,512]{1,0:T(8,128)}, f32[64,512]{1,0:T(8,128)}) custom-call(f32[64,512]{1,0:T(8,128)S(1)} %get-tuple-element.4.level, f32[5,64,128]{2,1,0:T(8,128)S(1)} %get-tuple-element.5.runoff), custom_call_target="tpu_custom_call" | custom-call | tf_op jit(solution)/shard_map/finish/pallas_call | solution.py:460

commit v7 on v5

--- a/solution.py
+++ b/solution.py
@@ -256,15 +256,13 @@
             final[w, pl.ds(base + r, 8), :] = new[1 + w]
         final[mid, pl.ds(base + r, 8), :] = jnp.where(lane < LANES // 2, new[-1], new[0])
 
-    def level_ring(step, carry):
-        for half in range(0, rows // 2, 8):
-            r = pl.multiple_of(step * (rows // 2), 8) + half
+    @pl.when(me_r >= 0)
+    def _():
+        for r in range(0, rows, 8):
             for w, value in enumerate(to_ring([final[w, pl.ds(base + r, 8), :] for w in inner_order])):
                 level[w, pl.ds(top + r, 8), :] = value
                 state[0, w, pl.ds(top + r, 8), :] = value
-        return carry
-
-    lax.fori_loop(0, 2, level_ring, 0)
+
     start_all(far_copies(level, 0))
 
     def ring_routes(first, last):
@@ -368,8 +366,8 @@
     def on_device(depth, rainfall, conveyance, flow_dir, outlet):
         rows, cols = depth.shape
         strips = cols // LANES
-        high = rows + 2 * MARGIN + 16
-        low = rows + 32
+        high = rows + 2 * MARGIN + 24
+        low = rows + 40
         f32 = functools.partial(pltpu.VMEM, dtype=jnp.float32)
         dma = pltpu.SemaphoreType.DMA
         segments = PASSES // MARGIN

time: 28.6 us -> 28 us (0.979)
  Pallas kernels: 27.8 us -> 27.1 us
    pallas_call x1, Pallas kernels: 26.8 us -> 26.1 us  [on_device(): pl.pallas_call(functools.partial(kernel, rows, cols, nrow, ncol), out_sha...]
where the time goes in v7:
time: 28 us; the launch traced here: 27.8 us
  Pallas kernels  27.1 us (97%)
  between operations  0.64 us (2%)
    pallas_call x1, Pallas kernels, on_device(): pl.pallas_call(functools.partial(kernel, rows, cols, nrow, ncol), out_sha...  26.1 us
    pallas_call x1, Pallas kernels, on_device(): pl.pallas_call(finish, out_shape=[jax.ShapeDtypeStruct((rows, cols), jnp....  1.02 us

profile of v7, /device:TPU:121, one launch (start us, length us, event | category | flops | bytes accessed | tf_op | source)
XLA Modules:
  0.0 27.8 jit_solution(13197679330763278484)
XLA Ops:
  0.6 26.1 %overland.1 = (f32[64,512]{1,0:T(8,128)S(1)}, f32[5,64,128]{2,1,0:T(8,128)S(1)}) custom-call(f32[64,512]{1,0:T(8,128)} %depth.1, f32[64,512]{1,0:T(8,128)} %rainfall.1, f32[64,512]{1,0:T(8,128)} %conveyance.1, s32[64,512]{1,0:T(8,128)} %flow_dir.1, s32[64,512]{1,0:T(8,128)} %outlet.1), custom_call_target="tpu_custom_call" | custom-call | tf_op jit(solution)/shard_map/overland/pallas_call | solution.py:376
  26.8 1.0 %finish.1 = (f32[64,512]{1,0:T(8,128)}, f32[64,512]{1,0:T(8,128)}) custom-call(f32[64,512]{1,0:T(8,128)S(1)} %get-tuple-element.4.level, f32[5,64,128]{2,1,0:T(8,128)S(1)} %get-tuple-element.5.runoff), custom_call_target="tpu_custom_call" | custom-call | tf_op jit(solution)/shard_map/finish/pallas_call | solution.py:409

commit v8 on v7

--- a/solution.py
+++ b/solution.py
@@ -185,7 +185,7 @@
             pack[1, w, pl.ds(8 + NEAR * (a - 1), 8), :] = near[a, w, pl.ds(base + rows - 8, 8), :]
 
     pl.semaphore_wait(barrier, neighbours)
-    start_all(near_copies)
+    start_all(near_copies[4:] + near_copies[:4])
     start_all(route_copies)
 
     def make_masks(target, codes, w, r):

time: 28 us -> 27.6 us (0.986)
  Pallas kernels: 27.1 us -> 26.7 us
    pallas_call x1, Pallas kernels: 26.1 us -> 25.7 us  [on_device(): pl.pallas_call(functools.partial(kernel, rows, cols, nrow, ncol), out_sha...]
where the time goes in v8:
time: 27.6 us; the launch traced here: 27.4 us
  Pallas kernels  26.7 us (97%)
  between operations  0.64 us (2%)
    pallas_call x1, Pallas kernels, on_device(): pl.pallas_call(functools.partial(kernel, rows, cols, nrow, ncol), out_sha...  25.7 us
    pallas_call x1, Pallas kernels, on_device(): pl.pallas_call(finish, out_shape=[jax.ShapeDtypeStruct((rows, cols), jnp....  1.02 us

profile of v8, /device:TPU:121, one launch (start us, length us, event | category | flops | bytes accessed | tf_op | source)
XLA Modules:
  0.0 27.4 jit_solution(16349670419140716710)
XLA Ops:
  0.6 25.7 %overland.1 = (f32[64,512]{1,0:T(8,128)S(1)}, f32[5,64,128]{2,1,0:T(8,128)S(1)}) custom-call(f32[64,512]{1,0:T(8,128)} %depth.1, f32[64,512]{1,0:T(8,128)} %rainfall.1, f32[64,512]{1,0:T(8,128)} %conveyance.1, s32[64,512]{1,0:T(8,128)} %flow_dir.1, s32[64,512]{1,0:T(8,128)} %outlet.1), custom_call_target="tpu_custom_call" | custom-call | tf_op jit(solution)/shard_map/overland/pallas_call | solution.py:376
  26.4 1.0 %finish.1 = (f32[64,512]{1,0:T(8,128)}, f32[64,512]{1,0:T(8,128)}) custom-call(f32[64,512]{1,0:T(8,128)S(1)} %get-tuple-element.4.level, f32[5,64,128]{2,1,0:T(8,128)S(1)} %get-tuple-element.5.runoff), custom_call_target="tpu_custom_call" | custom-call | tf_op jit(solution)/shard_map/finish/pallas_call | solution.py:409

commit v9 on v8

--- a/solution.py
+++ b/solution.py
@@ -11,6 +11,8 @@
 SUBSTEPS = 3
 PASSES = 64
 MARGIN = 32
+HALF = MARGIN // 2
+LAG = 8
 LANES = 128
 NEAR = 4
 MESH = pl.DeviceIdType.MESH
@@ -160,11 +162,15 @@
         route_mid_copies.append(remote(
             (dr, dc), route.at[mid, source, :], route.at[mid, target, :], route_ssem.at[1, d], route_rsem.at[1, d]))
 
-    def far_copies(source, seg):
-        return [
-            remote((dr, dc), source.at[:, edge[dr][0], :], far.at[seg, 1 - d], far_ssem.at[seg, d], far_rsem.at[seg, d])
-            for d, (dr, dc) in enumerate(VERTICAL)
-        ]
+    def far_copies(source, seg, part):
+        made = []
+        for d, (dr, dc) in enumerate(VERTICAL):
+            at = part * HALF if dr < 0 else (1 - part) * HALF
+            made.append(remote(
+                (dr, dc), source.at[:, pl.ds(at + (top if dr < 0 else end - MARGIN), HALF), :],
+                far.at[seg, 1 - d, :, pl.ds(at, HALF), :],
+                far_ssem.at[seg, 2 * part + d], far_rsem.at[seg, 2 * part + d]))
+        return made
 
     for load in loads:
         load.wait()
@@ -263,7 +269,8 @@
                 level[w, pl.ds(top + r, 8), :] = value
                 state[0, w, pl.ds(top + r, 8), :] = value
 
-    start_all(far_copies(level, 0))
+    start_all(far_copies(level, 0, 0))
+    start_all(far_copies(level, 0, 1))
 
     def ring_routes(first, last):
         for r in range(first, last, 8):
@@ -290,21 +297,23 @@
             if p == MARGIN - 1:
                 state[0, :, here, :] = value
 
-    def halo(seg, half):
-        first = end if half else top - MARGIN
-        for w in inner_order:
-            for r in range(0, MARGIN, 8):
-                state[0, w, pl.ds(first + r, 8), :] = far[seg, half, w, pl.ds(r, 8), :]
-
-        @pl.when(seg == 0)
-        def _():
-            for w in inner_order:
-                for r in range(0, MARGIN, 8):
-                    level[w, pl.ds(first + r, 8), :] = far[0, half, w, pl.ds(r, 8), :]
-
-    def bands():
-        for p in range(MARGIN):
-            one_pass(p, starts(top - MARGIN + p + 1, top + p + 1) + starts(end - p - 1, end + MARGIN - p - 1))
+    def receive(seg, part):
+        arrive_all(far_copies(level, seg, part))
+        for half in range(2):
+            at = part * HALF if half else (1 - part) * HALF
+            first = end if half else top - MARGIN
+            for r in range(at, at + HALF, 8):
+                for w in inner_order:
+                    state[0, w, pl.ds(first + r, 8), :] = far[seg, half, w, pl.ds(r, 8), :]
+                    if seg == 0:
+                        level[w, pl.ds(first + r, 8), :] = far[seg, half, w, pl.ds(r, 8), :]
+
+    def inner(p):
+        return starts(top - HALF + p + 1, top + p + 1) + starts(end - p - 1, end + HALF - p - 1)
+
+    def outer(p):
+        return (starts(top - MARGIN + p + 1, top - HALF + p + 1)
+                + starts(end + HALF - p - 1, end + MARGIN - p - 1))
 
     def segment(seg, carry):
         for p in range(rows // 2 - 1):
@@ -320,16 +329,28 @@
             for w in inner_order:
                 for r in (*range(top - MARGIN, top + 8, 8), *range(end - 8, end + MARGIN, 8)):
                     make_masks(masks, ring_route, w, r)
-
-        arrive_all(far_copies(level, seg))
-        leave_all(far_copies(level, seg))
-        halo(seg, 0)
-        halo(seg, 1)
-        bands()
-
-        @pl.when(seg == 0)
+            receive(0, 0)
+            for p in range(MARGIN + LAG):
+                if p == LAG:
+                    receive(0, 1)
+                if p < MARGIN:
+                    one_pass(p, inner(p))
+                if p >= LAG:
+                    one_pass(p - LAG, outer(p - LAG))
+                if p == MARGIN - 1:
+                    start_all(far_copies(state.at[MARGIN], 1, 1))
+            start_all(far_copies(state.at[MARGIN], 1, 0))
+            for part in range(2):
+                leave_all(far_copies(level, 0, part))
+
+        @pl.when(seg == 1)
         def _():
-            start_all(far_copies(state.at[MARGIN], 1))
+            receive(1, 1)
+            receive(1, 0)
+            for part in range(2):
+                leave_all(far_copies(level, 1, part))
+            for p in range(MARGIN):
+                one_pass(p, inner(p) + outer(p))
 
         return carry
 
@@ -400,7 +421,7 @@
                 f32((strips + 3, low, LANES)),
                 dma((5,)),
                 dma((8,)), dma((8,)), dma((2, 2)), dma((2, 2)),
-                dma((segments, 2)), dma((segments, 2)),
+                dma((segments, 4)), dma((segments, 4)),
             ],
             compiler_params=pltpu.CompilerParams(
                 collective_id=0, has_side_effects=True, vmem_limit_bytes=32 * 2**20),

time: 27.6 us -> 27.3 us (0.989)
  no operation moved by 1% of the time
where the time goes in v9:
time: 27.3 us; the launch traced here: 27.2 us
  Pallas kernels  26.6 us (97%)
  between operations  0.64 us (2%)
    pallas_call x1, Pallas kernels, on_device(): pl.pallas_call(functools.partial(kernel, rows, cols, nrow, ncol), out_sha...  25.5 us
    pallas_call x1, Pallas kernels, on_device(): pl.pallas_call(finish, out_shape=[jax.ShapeDtypeStruct((rows, cols), jnp....  1.02 us

profile of v9, /device:TPU:121, one launch (start us, length us, event | category | flops | bytes accessed | tf_op | source)
XLA Modules:
  0.0 27.2 jit_solution(14632695948513819601)
XLA Ops:
  0.6 25.5 %overland.1 = (f32[64,512]{1,0:T(8,128)S(1)}, f32[5,64,128]{2,1,0:T(8,128)S(1)}) custom-call(f32[64,512]{1,0:T(8,128)} %depth.1, f32[64,512]{1,0:T(8,128)} %rainfall.1, f32[64,512]{1,0:T(8,128)} %conveyance.1, s32[64,512]{1,0:T(8,128)} %flow_dir.1, s32[64,512]{1,0:T(8,128)} %outlet.1), custom_call_target="tpu_custom_call" | custom-call | tf_op jit(solution)/shard_map/overland/pallas_call | solution.py:397
  26.2 1.0 %finish.1 = (f32[64,512]{1,0:T(8,128)}, f32[64,512]{1,0:T(8,128)}) custom-call(f32[64,512]{1,0:T(8,128)S(1)} %get-tuple-element.4.level, f32[5,64,128]{2,1,0:T(8,128)S(1)} %get-tuple-element.5.runoff), custom_call_target="tpu_custom_call" | custom-call | tf_op jit(solution)/shard_map/finish/pallas_call | solution.py:430

commit v10 on v9

--- a/solution.py
+++ b/solution.py
@@ -262,15 +262,17 @@
             final[w, pl.ds(base + r, 8), :] = new[1 + w]
         final[mid, pl.ds(base + r, 8), :] = jnp.where(lane < LANES // 2, new[-1], new[0])
 
-    @pl.when(me_r >= 0)
-    def _():
-        for r in range(0, rows, 8):
-            for w, value in enumerate(to_ring([final[w, pl.ds(base + r, 8), :] for w in inner_order])):
-                level[w, pl.ds(top + r, 8), :] = value
-                state[0, w, pl.ds(top + r, 8), :] = value
-
-    start_all(far_copies(level, 0, 0))
-    start_all(far_copies(level, 0, 1))
+    for part, blocks in enumerate((
+        (*range(0, HALF, 8), *range(rows - HALF, rows, 8)), range(HALF, rows - HALF, 8),
+    )):
+        @pl.when(me_r >= 0)
+        def _():
+            for r in blocks:
+                for w, value in enumerate(to_ring([final[w, pl.ds(base + r, 8), :] for w in inner_order])):
+                    level[w, pl.ds(top + r, 8), :] = value
+                    state[0, w, pl.ds(top + r, 8), :] = value
+
+        start_all(far_copies(level, 0, part))
 
     def ring_routes(first, last):
         for r in range(first, last, 8):

time: 27.3 us -> 27.4 us (level)
  no operation moved by 1% of the time
where the time goes in v10:
time: 27.4 us; the launch traced here: 27.3 us
  Pallas kernels  26.6 us (97%)
  between operations  0.64 us (2%)
    pallas_call x1, Pallas kernels, on_device(): pl.pallas_call(functools.partial(kernel, rows, cols, nrow, ncol), out_sha...  25.6 us
    pallas_call x1, Pallas kernels, on_device(): pl.pallas_call(finish, out_shape=[jax.ShapeDtypeStruct((rows, cols), jnp....  1.02 us

profile of v10, /device:TPU:121, one launch (start us, length us, event | category | flops | bytes accessed | tf_op | source)
XLA Modules:
  0.0 27.3 jit_solution(16612995710149897062)
XLA Ops:
  0.6 25.6 %overland.1 = (f32[64,512]{1,0:T(8,128)S(1)}, f32[5,64,128]{2,1,0:T(8,128)S(1)}) custom-call(f32[64,512]{1,0:T(8,128)} %depth.1, f32[64,512]{1,0:T(8,128)} %rainfall.1, f32[64,512]{1,0:T(8,128)} %conveyance.1, s32[64,512]{1,0:T(8,128)} %flow_dir.1, s32[64,512]{1,0:T(8,128)} %outlet.1), custom_call_target="tpu_custom_call" | custom-call | tf_op jit(solution)/shard_map/overland/pallas_call | solution.py:399
  26.2 1.0 %finish.1 = (f32[64,512]{1,0:T(8,128)}, f32[64,512]{1,0:T(8,128)}) custom-call(f32[64,512]{1,0:T(8,128)S(1)} %get-tuple-element.4.level, f32[5,64,128]{2,1,0:T(8,128)S(1)} %get-tuple-element.5.runoff), custom_call_target="tpu_custom_call" | custom-call | tf_op jit(solution)/shard_map/finish/pallas_call | solution.py:432
